TPU v7x, 8 devices: a whole 2x2x1 slice. The times are simulated.
8 devices in a mesh: dp: 2 (over z, y), ep: 4 (over x, core).
Axes of the slice: x: 2, y: 2, z: 1, core: 2. Of those that a mesh axis runs over, the one named last changes fastest.
Arguments:
- grad_y: bfloat16 [512, 1024], P(('dp', 'ep')), parts along dimension 0
- gate_vals: float32 [512, 8], P(('dp', 'ep')), parts along dimension 0
- topk_idx: int32 [512, 8], P(('dp', 'ep')), parts along dimension 0
- slot_ids: int32 [512, 8], P(('dp', 'ep')), parts along dimension 0
- pair_counts: int32 [8, 32], P(('dp', 'ep')), parts along dimension 0
- y_routed: bfloat16 [512, 8, 1024], P(('dp', 'ep')), parts along dimension 0
- x_disp: bfloat16 [64, 128, 1024], P(('dp', 'ep')), parts along dimension 0
- h_gate: bfloat16 [64, 128, 512], P(('dp', 'ep')), parts along dimension 0
- h_up: bfloat16 [64, 128, 512], P(('dp', 'ep')), parts along dimension 0
- w_gate: bfloat16 [32, 1024, 512], P('ep')
- w_up: bfloat16 [32, 1024, 512], P('ep')
- w_down: bfloat16 [32, 512, 1024], P('ep')
Outputs:
- output 1: bfloat16 [512, 1024], P(('dp', 'ep')), parts along dimension 0
- output 2: float32 [512, 8], P(('dp', 'ep')), parts along dimension 0
- output 3: float32 [64, 1024, 512], P(('dp', 'ep')), parts along dimension 0
- output 4: float32 [64, 1024, 512], P(('dp', 'ep')), parts along dimension 0
- output 5: float32 [64, 512, 1024], P(('dp', 'ep')), parts along dimension 0
There are 2 independent parts. A program takes and returns all parts, laid end to end along the dimension named above; an argument that names none is the same for every part.
All inputs are finite; a program needn't handle non-finite values.
Results may differ from a plain program's by a relative error of at most 0.0149174.
Values are sent between devices in bfloat16 or wider.
A program may use at most 1 GiB of HBM per device.

v0:
```python
import jax
import jax.numpy as jnp
from jax import lax
from jax.sharding import PartitionSpec as P


def build_send(grad_y, gate_vals, topk_idx, slot_ids, n_exp, cap_rows):
    tok_dev, top_k = topk_idx.shape
    dest_row = jnp.where(slot_ids >= 0, topk_idx * cap_rows + slot_ids, n_exp * cap_rows).reshape(-1)
    row_source = jnp.full((n_exp * cap_rows,), tok_dev * top_k, jnp.int32).at[dest_row].set(jnp.arange(tok_dev * top_k, dtype=jnp.int32), mode="drop")
    dy_rows = jnp.take(grad_y, row_source // top_k, axis=0, mode="fill", fill_value=0)
    gate_rows = jnp.take(gate_vals.reshape(-1), row_source, mode="fill", fill_value=0)
    return (gate_rows[:, None] * dy_rows).astype(jnp.bfloat16).reshape(n_exp, cap_rows, grad_y.shape[1])


def gather_back(ret_rows, topk_idx, slot_ids, cap_rows):
    tok_dev, top_k = topk_idx.shape
    src_row = jnp.where(slot_ids >= 0, topk_idx * cap_rows + slot_ids, ret_rows.shape[0]).reshape(-1)
    picked = jnp.take(ret_rows, src_row, axis=0, mode="fill", fill_value=0).reshape(tok_dev, top_k, ret_rows.shape[1])
    return jnp.sum(picked, axis=1, dtype=jnp.float32).astype(jnp.bfloat16)


def expert_grads(grad_rows, x_rows, hg_rows, hu_rows, w_gate, w_up, w_down):
    grad_hidden = jnp.einsum("erd,efd->erf", grad_rows, w_down, preferred_element_type=jnp.float32).astype(jnp.bfloat16)
    gate_f = hg_rows.astype(jnp.float32)
    up_f = hu_rows.astype(jnp.float32)
    gate_sig = jax.nn.sigmoid(gate_f)
    gate_act = gate_f * gate_sig
    hidden_act = (gate_act * up_f).astype(jnp.bfloat16)
    grad_h = grad_hidden.astype(jnp.float32)
    grad_hgate = (grad_h * up_f * gate_sig * (1.0 + gate_f * (1.0 - gate_sig))).astype(jnp.bfloat16)
    grad_hup = (grad_h * gate_act).astype(jnp.bfloat16)
    grad_wdown = jnp.einsum("erf,erd->efd", hidden_act, grad_rows, preferred_element_type=jnp.float32)
    grad_wgate = jnp.einsum("erd,erf->edf", x_rows, grad_hgate, preferred_element_type=jnp.float32)
    grad_wup = jnp.einsum("erd,erf->edf", x_rows, grad_hup, preferred_element_type=jnp.float32)
    grad_disp = (jnp.einsum("erf,edf->erd", grad_hgate, w_gate, preferred_element_type=jnp.float32) + jnp.einsum("erf,edf->erd", grad_hup, w_up, preferred_element_type=jnp.float32)).astype(jnp.bfloat16)
    return grad_disp, grad_wgate, grad_wup, grad_wdown


def solution(mesh):
    n_dev = mesh.shape["ep"]
    rows_spec = P(("dp", "ep"), None)
    cube_spec = P(("dp", "ep"), None, None)
    weight_spec = P("ep", None, None)

    def local_step(grad_y, gate_vals, topk_idx, slot_ids, pair_counts, y_routed, x_disp, h_gate, h_up, w_gate, w_up, w_down):
        n_loc = w_gate.shape[0]
        n_exp = n_loc * n_dev
        cap_rows = x_disp.shape[1] // n_dev
        model_dim = grad_y.shape[1]
        grad_gate = jnp.einsum("td,tkd->tk", grad_y, y_routed, preferred_element_type=jnp.float32)
        send_rows = build_send(grad_y, gate_vals, topk_idx, slot_ids, n_exp, cap_rows)
        recv_rows = lax.all_to_all(send_rows.reshape(n_dev, n_loc, cap_rows, model_dim), "ep", 0, 1)
        recv_counts = lax.all_to_all(pair_counts.reshape(n_dev, n_loc), "ep", 0, 1)
        keep_row = lax.broadcasted_iota(jnp.int32, (n_loc, n_dev, cap_rows), 2) < recv_counts[:, :, None]
        grad_rows = jnp.where(keep_row[..., None], recv_rows, jnp.zeros((), jnp.bfloat16)).reshape(n_loc, n_dev * cap_rows, model_dim)
        grad_disp, grad_wgate, grad_wup, grad_wdown = expert_grads(grad_rows, x_disp, h_gate, h_up, w_gate, w_up, w_down)
        ret_rows = lax.all_to_all(grad_disp.reshape(n_loc, n_dev, cap_rows, model_dim), "ep", 1, 0)
        grad_x = gather_back(ret_rows.reshape(n_exp * cap_rows, model_dim), topk_idx, slot_ids, cap_rows)
        return grad_x, grad_gate, grad_wgate, grad_wup, grad_wdown

    return jax.shard_map(local_step, mesh=mesh, in_specs=(rows_spec, rows_spec, rows_spec, rows_spec, rows_spec, cube_spec, cube_spec, cube_spec, cube_spec, weight_spec, weight_spec, weight_spec), out_specs=(rows_spec, rows_spec, cube_spec, cube_spec, cube_spec), check_vma=False)
```

profile of v0, /device:TPU:0, one launch (start us, length us, event | category | flops | bytes accessed | tf_op | source)
XLA Modules:
  0.0 156.5 jit_solution(1386949907372114062)
XLA Ops:
  0.6 0.0 copy-start
  0.6 0.5 broadcast.117
  1.2 1.4 reduce.4
  2.6 0.7 broadcast_in_dim_reshape.6
  3.3 4.6 %all-to-all-start = ((s32[4,8,1]{1,2,0:T(1,128)}), s32[4,8,1]{1,2,0:T(1,128)S(1)}, u32[]{:S(2)}, u32[]{:S(2)}) async-start(s32[4,8,1]{1,2,0:T(1,128)} %bitcast), calls=%async_computation | async-start | bytes 4096 | tf_op jit(solution)/shard_map/all_to_all | solution.py:54
  7.9 0.7 compare_and_fusion.1
  8.6 0.1 copy.52
  8.7 0.1 reshape.115
  8.8 2.4 %scatter_custom_fusion = s32[1024]{0:T(1024)S(1)} fusion(s32[512]{0:T(512)S(1)} %bitcast.43, s32[512]{0:T(512)S(1)} %iota.18, s32[]{:T(128)} %constant.61.clone.1), kind=kCustom, calls=%fused_computation.51 | custom fusion | bytes 4100 | tf_op jit(solution)/shard_map/scatter | solution.py:10
  11.3 0.8 copy.53
  12.0 0.1 reshape.116
  12.1 0.0 copy-start.1
  12.1 6.9 %gather_fusion = f32[1024]{0:T(1024)S(1)} fusion(f32[512]{0:T(512)S(1)} %reshape.116, s32[1024]{0:T(1024)S(1)} %get-tuple-element.27), kind=kCustom, calls=%fused_computation | custom fusion | bytes 12288 | tf_op jit(solution)/shard_map/jit(_take)/gather | solution.py:12
  19.0 0.1 mul.43
  19.1 0.1 broadcast_in_dim.61
  19.2 0.0 copy-done.1
  19.2 5.3 %gather_fusion.1 = bf16[1024,1024]{1,0:T(8,128)(2,1)} fusion(bf16[64,1024]{1,0:T(8,128)(2,1)S(1)} %copy-done.1, s32[1024]{0:T(1024)S(1)} %get-tuple-element.28), kind=kCustom, calls=%fused_computation.1 | custom fusion | bytes 4198400 | tf_op jit(solution)/shard_map/jit(_take)/gather | solution.py:11
  24.5 3.5 %multiply_convert_fusion = bf16[4,8,1,32,1024]{4,3,1,2,0:T(8,128)(2,1)} fusion(bf16[4,8,1,32,1024]{4,3,1,2,0:T(8,128)(2,1)} %bitcast.38, f32[4,8,32]{2,1,0:T(8,128)S(1)} %mul.43, pred[4,8,32]{2,1,0:T(8,128)(4,1)S(1)} %broadcast_in_dim.61), kind=kLoop, calls=%fused_computation.7 | loop fusion | flops 4194304 | bytes 4199424 | tf_op jit(solution)/shard_map/convert_element_type | solution.py:13
  28.0 0.0 all-to-all-done
  28.0 4.4 %all-to-all-start.1 = ((bf16[4,8,1,32,1024]{4,3,1,2,0:T(8,128)(2,1)}), bf16[4,8,1,32,1024]{4,3,1,2,0:T(8,128)(2,1)}, u32[]{:S(2)}, u32[]{:S(2)}) async-start(bf16[4,8,1,32,1024]{4,3,1,2,0:T(8,128)(2,1)} %multiply_convert_fusion), calls=%async_computation.1 | async-start | bytes 4194304 | tf_op jit(solution)/shard_map/all_to_all | solution.py:53
  32.5 0.1 iota.16
  32.6 0.1 copy.49
  32.7 2.0 %fusion.16 = f32[64,1,8]{2,1,0:T(1,128)S(1)} fusion(bf16[64,8,1024]{2,1,0:T(8,128)(2,1)} %param.17, bf16[64,1024,1]{1,0,2:T(8,128)(2,1)S(1)} %bitcast.37), kind=kOutput, calls=%fused_computation.31 | convolution fusion | flops 1048576 | bytes 1181696 | tf_op jit(solution)/shard_map/td,tkd->tk/dot_general | solution.py:51
  34.6 0.7 copy.63
  35.3 0.1 copy.51
  35.4 0.1 lt.54
  35.5 0.1 lt.55
  35.5 22.3 %all-to-all-done.1 = bf16[4,8,1,32,1024]{4,3,1,2,0:T(8,128)(2,1)} async-done(((bf16[4,8,1,32,1024]{4,3,1,2,0:T(8,128)(2,1)}), bf16[4,8,1,32,1024]{4,3,1,2,0:T(8,128)(2,1)}, u32[]{:S(2)}, u32[]{:S(2)}) %all-to-all-start.1) | async-done | bytes 2097184 | tf_op jit(solution)/shard_map/all_to_all | solution.py:53
  57.9 1.8 %copy.55 = bf16[4,8,1,32,1024]{4,3,0,1,2:T(8,128)(2,1)S(1)} copy(bf16[4,8,1,32,1024]{4,3,1,2,0:T(8,128)(2,1)} %all-to-all-done.1) | data formatting | bytes 4194304 | tf_op jit(solution)/shard_map/all_to_all | solution.py:53
  59.6 0.0 copy-start.3
  59.7 1.3 copy-done.3
  61.0 0.0 copy-start.2
  61.0 0.0 copy-start.5
  61.0 0.0 slice-start
  61.0 6.4 %fusion.11 = bf16[8,128,512]{2,1,0:T(8,128)(2,1)S(1)} fusion(bf16[8,512,1024]{2,1,0:T(8,128)(2,1)} %param.23, bf16[8,128,1024]{2,1,0:T(8,128)(2,1)S(1)} %bitcast.39, pred[8,128]{1,0:T(8,128)(4,1)S(1)} %broadcast_compare_fusion), kind=kOutput, calls=%fused_computation.26 | convolution fusion | flops 1075314688 | bytes 11535360 | tf_op jit(solution)/shard_map/erd,efd->erf/dot_general | solution.py:24
  67.4 0.0 copy-done.2
  67.5 0.0 copy-done.5
  67.5 0.0 copy-start.4
  67.5 0.0 slice-start.1
  67.5 8.7 %fusion.29 = f32[8,128,1024]{2,1,0:T(8,128)} fusion(bf16[8,1024,512]{2,1,0:T(8,128)(2,1)} %param.21, bf16[8,128,512]{2,1,0:T(8,128)(2,1)S(1)} %copy-done.5, bf16[8,128,512]{2,1,0:T(8,128)(2,1)S(1)} %fusion.11, bf16[8,128,512]{2,1,0:T(8,128)(2,1)S(1)} %copy-done.2), kind=kOutput, calls=%fused_computation.57 | convolution fusion | flops 1080557568 | bytes 15728640 | tf_op jit(solution)/shard_map/erf,edf->erd/dot_general | solution.py:36
  76.2 0.0 copy-done.4
  76.2 0.0 slice-done
  76.2 0.0 slice-done.1
  76.2 5.1 %add_convert_fusion = bf16[8,128,1024]{2,1,0:T(8,128)(2,1)S(1)} fusion(f32[8,128,1024]{2,1,0:T(8,128)} %fusion.29, bf16[8,1024,512]{2,1,0:T(8,128)(2,1)S(1)} %bitcast.47, bf16[8,128,512]{2,1,0:T(8,128)(2,1)S(1)} %fusion.11, bf16[8,128,512]{2,1,0:T(8,128)(2,1)S(1)} %copy-done.2), kind=kOutput, calls=%fused_computation.6 | convolution fusion | flops 1080033280 | bytes 16777216 | tf_op jit(solution)/shard_map/erf,edf->erd/dot_general | solution.py:36
  81.3 1.6 copy.56
  82.8 4.6 %all-to-all-start.2 = ((bf16[1,8,4,32,1024]{4,3,1,0,2:T(8,128)(2,1)}), bf16[1,8,4,32,1024]{4,3,1,0,2:T(8,128)(2,1)}, u32[]{:S(2)}, u32[]{:S(2)}) async-start(bf16[1,8,4,32,1024]{4,3,1,0,2:T(8,128)(2,1)} %copy.56), calls=%async_computation.2 | async-start | bytes 4194304 | tf_op jit(solution)/shard_map/all_to_all | solution.py:58
  87.4 0.0 copy-done
  87.4 10.1 %convolution_bitcast_fusion.1 = f32[8,1024,512]{1,2,0:T(8,128)} fusion(bf16[8,128,1024]{2,1,0:T(8,128)(2,1)S(1)} %copy-done, bf16[8,128,512]{2,1,0:T(8,128)(2,1)} %param.20, bf16[8,128,512]{2,1,0:T(8,128)(2,1)} %copy-done.4, bf16[8,128,512]{2,1,0:T(8,128)(2,1)S(1)} %copy-done.2), kind=kOutput, calls=%fused_computation.5 | convolution fusion | flops 1080557568 | bytes 22020096 | tf_op jit(solution)/shard_map/erd,erf->edf/dot_general | solution.py:34
  97.6 16.4 %copy.60 = f32[8,1024,512]{2,1,0:T(8,128)} copy(f32[8,1024,512]{1,2,0:T(8,128)} %convolution_bitcast_fusion.1) | data formatting | bytes 33554432
  114.0 9.8 %convolution_bitcast_fusion = f32[8,1024,512]{1,2,0:T(8,128)} fusion(bf16[8,128,1024]{2,1,0:T(8,128)(2,1)S(1)} %copy-done, bf16[8,128,512]{2,1,0:T(8,128)(2,1)} %copy-done.4, bf16[8,128,512]{2,1,0:T(8,128)(2,1)S(1)} %copy-done.2), kind=kOutput, calls=%fused_computation.4 | convolution fusion | flops 1077936128 | bytes 20971520 | tf_op jit(solution)/shard_map/erd,erf->edf/dot_general | solution.py:35
  123.8 16.4 %copy.61 = f32[8,1024,512]{2,1,0:T(8,128)} copy(f32[8,1024,512]{1,2,0:T(8,128)} %convolution_bitcast_fusion) | data formatting | bytes 33554432
  140.2 10.5 %fusion.9 = f32[8,512,1024]{2,1,0:T(8,128)} fusion(bf16[8,128,1024]{2,1,0:T(8,128)(2,1)} %bitcast.40, pred[8,128]{1,0:T(8,128)(4,1)S(1)} %broadcast_compare_fusion, bf16[8,128,512]{2,1,0:T(8,128)(2,1)} %param.20, bf16[8,128,512]{2,1,0:T(8,128)(2,1)S(1)} %copy-done.2), kind=kOutput, calls=%fused_computation.24 | convolution fusion | flops 1078984704 | bytes 20972544 | tf_op jit(solution)/shard_map/erf,erd->efd/dot_general | solution.py:33
  150.7 0.0 all-to-all-done.2
  150.7 4.6 %gather_fusion.2 = bf16[512,1024]{1,0:T(8,128)(2,1)S(1)} fusion(bf16[1024,1024]{1,0:T(8,128)(2,1)} %bitcast.13, s32[1024]{0:T(1024)S(1)} %pad_clamp_fusion), kind=kCustom, calls=%fused_computation.2 | custom fusion | bytes 2099200 | tf_op jit(solution)/shard_map/jit(_take)/gather | solution.py:19
  155.3 1.2 fusion.13
  (9 shorter events, 0.1 us)
Async XLA Ops:
  0.6 86.8 %copy-start = (bf16[8,128,1024]{2,1,0:T(8,128)(2,1)S(1)}, bf16[8,128,1024]{2,1,0:T(8,128)(2,1)}, u32[]{:S(2)}) copy-start(bf16[8,128,1024]{2,1,0:T(8,128)(2,1)} %param.18) | copy-start | bytes 6291460
  3.3 24.8 %all-to-all-start = ((s32[4,8,1]{1,2,0:T(1,128)}), s32[4,8,1]{1,2,0:T(1,128)S(1)}, u32[]{:S(2)}, u32[]{:S(2)}) async-start(s32[4,8,1]{1,2,0:T(1,128)} %bitcast), calls=%async_computation | async-start | bytes 4096 | tf_op jit(solution)/shard_map/all_to_all | solution.py:54
  12.1 7.1 %copy-start.1 = (bf16[64,1024]{1,0:T(8,128)(2,1)S(1)}, bf16[64,1024]{1,0:T(8,128)(2,1)}, u32[]{:S(2)}) copy-start(bf16[64,1024]{1,0:T(8,128)(2,1)} %param.12) | copy-start | bytes 393220
  28.0 29.9 %all-to-all-start.1 = ((bf16[4,8,1,32,1024]{4,3,1,2,0:T(8,128)(2,1)}), bf16[4,8,1,32,1024]{4,3,1,2,0:T(8,128)(2,1)}, u32[]{:S(2)}, u32[]{:S(2)}) async-start(bf16[4,8,1,32,1024]{4,3,1,2,0:T(8,128)(2,1)} %multiply_convert_fusion), calls=%async_computation.1 | async-start | bytes 4194304 | tf_op jit(solution)/shard_map/all_to_all | solution.py:53
  59.6 1.3 copy-start.3
  61.0 6.5 %copy-start.2 = (bf16[8,128,512]{2,1,0:T(8,128)(2,1)S(1)}, bf16[8,128,512]{2,1,0:T(8,128)(2,1)}, u32[]{:S(2)}) copy-start(bf16[8,128,512]{2,1,0:T(8,128)(2,1)} %param.19) | copy-start | bytes 3145732
  61.0 6.5 %copy-start.5 = (bf16[8,128,512]{2,1,0:T(8,128)(2,1)S(1)}, bf16[8,128,512]{2,1,0:T(8,128)(2,1)}, u32[]{:S(2)}) copy-start(bf16[8,128,512]{2,1,0:T(8,128)(2,1)} %param.20) | copy-start | bytes 3145732
  61.0 15.2 %slice-start = ((s8[8388608]{0:T(1024)(128)(4,1)}), s8[4194304]{0:T(1024)(128)(4,1)S(1)}, s32[]{:S(2)}) async-start(s8[8388608]{0:T(1024)(128)(4,1)} %bitcast.46), calls=%async_computation.3 | async-start | bytes 8388608
  67.5 8.7 %copy-start.4 = (bf16[8,128,512]{2,1,0:T(8,128)(2,1)}, bf16[8,128,512]{2,1,0:T(8,128)(2,1)S(1)}, u32[]{:S(2)}) copy-start(bf16[8,128,512]{2,1,0:T(8,128)(2,1)S(1)} %fusion.11) | copy-start | bytes 3145732
  67.5 8.7 %slice-start.1 = ((s8[8388608]{0:T(1024)(128)(4,1)}), s8[4194304]{0:T(1024)(128)(4,1)S(1)}, s32[]{:S(2)}) async-start(s8[8388608]{0:T(1024)(128)(4,1)} %bitcast.46), calls=%async_computation.4 | async-start | bytes 8388608
  82.8 67.9 %all-to-all-start.2 = ((bf16[1,8,4,32,1024]{4,3,1,0,2:T(8,128)(2,1)}), bf16[1,8,4,32,1024]{4,3,1,0,2:T(8,128)(2,1)}, u32[]{:S(2)}, u32[]{:S(2)}) async-start(bf16[1,8,4,32,1024]{4,3,1,0,2:T(8,128)(2,1)} %copy.56), calls=%async_computation.2 | async-start | bytes 4194304 | tf_op jit(solution)/shard_map/all_to_all | solution.py:58
where the time goes:
time: 158 us; the launch traced here: 156 us
  local copies, waits for them, and re-layouts  60.2 us (38%)
  matrix products  52.5 us (33%)
  waiting for transfers between devices  22.3 us (14%)
  starting transfers between devices  13.7 us (9%)
  other arithmetic  6.9 us (4%)
    unnamed x20, local copies, waits for them, and re-layouts  35.5 us
    all_to_all x1, waiting for transfers between devices, local_step(): lax.all_to_all(send_rows.reshape(n_dev, n_loc, cap_rows, model_dim), 'ep'...  22.3 us
    dot_general x1, matrix products, expert_grads(): jnp.einsum('erf,erd->efd', hidden_act, grad_rows, preferred_element_type=...  10.5 us
    dot_general x1, matrix products, expert_grads(): jnp.einsum('erd,erf->edf', x_rows, grad_hgate, preferred_element_type=jnp...  10.1 us
    dot_general x1, matrix products, expert_grads(): jnp.einsum('erd,erf->edf', x_rows, grad_hup, preferred_element_type=jnp.f...  9.79 us
    dot_general x1, matrix products, expert_grads(): jnp.einsum('erf,edf->erd', grad_hgate, w_gate, preferred_element_type=jnp...  8.67 us
    gather x1, local copies, waits for them, and re-layouts, build_send(): jnp.take(gate_vals.reshape(-1), row_source, mode='fill', fill_value=0)  6.87 us
    dot_general x1, matrix products, expert_grads(): jnp.einsum('erd,efd->erf', grad_rows, w_down, preferred_element_type=jnp....  6.45 us
  transfers between devices with their start and end apart: 3, of which 1 were waited for; matrix products, arithmetic and copies ran while one was open for 55% of the time, Pallas kernels for 0%

commit v1 on v0

v1 whole, which is shorter than its diff:
```python
import jax
import jax.numpy as jnp
from jax import lax
from jax.experimental import pallas as pl
from jax.experimental.pallas import tpu as pltpu
from jax.sharding import PartitionSpec as P

MESH_ID = pl.DeviceIdType.MESH
F32 = jnp.float32
BF16 = jnp.bfloat16
NT = (((1,), (1,)), ((), ()))
TN = (((0,), (0,)), ((), ()))


def token_kernel(gy, gv, tk, sl, pc, yr, hg, hu, wg, wu, wd,
                 part, dd, aa, dh, gg,
                 gy_all, gv_all, tk_all, sl_all, pc_all, yr_v, hg_v, hu_v, wg_v, wu_v, wd_v,
                 c1_v, s_v, p_all, r_all,
                 own_sem, bulk_sem, wd_sem, wg_sem, wu_sem,
                 gs_sem, gr_sem, ss_sem, sr_sem):
    n_loc = wd.shape[0]
    cap = dd.shape[2]
    tok, dim = gy.shape
    ffn = wd.shape[1]
    half = tok // 2
    me = lax.axis_index("ep")
    partner = me + 1 - 2 * lax.rem(me, 2)
    far = lax.rem(me + 2, 4)
    far_partner = lax.rem(partner + 2, 4)
    peers = (partner, far, far_partner)

    own = [pltpu.make_async_copy(gy, gy_all.at[me], own_sem.at[0]),
           pltpu.make_async_copy(gv, gv_all.at[me], own_sem.at[1]),
           pltpu.make_async_copy(tk, tk_all.at[me], own_sem.at[2]),
           pltpu.make_async_copy(sl, sl_all.at[me], own_sem.at[3]),
           pltpu.make_async_copy(pc, pc_all.at[me], own_sem.at[4])]
    for c in own:
        c.start()
    barrier = pltpu.get_barrier_semaphore()
    for d in peers:
        pl.semaphore_signal(barrier, inc=1, device_id={"ep": d}, device_id_type=MESH_ID)
    bulk = [pltpu.make_async_copy(hg, hg_v, bulk_sem.at[0]),
            pltpu.make_async_copy(hu, hu_v, bulk_sem.at[1]),
            pltpu.make_async_copy(yr, yr_v, bulk_sem.at[2])]
    for c in bulk:
        c.start(priority=1)
    for e in range(n_loc):
        pltpu.make_async_copy(wd.at[e], wd_v.at[e], wd_sem.at[e]).start(priority=1)
    for e in range(n_loc):
        pltpu.make_async_copy(wg.at[e], wg_v.at[e], wg_sem.at[e]).start(priority=1)
        pltpu.make_async_copy(wu.at[e], wu_v.at[e], wu_sem.at[e]).start(priority=1)
    for c in own:
        c.wait()
    pl.semaphore_wait(barrier, 3)

    def remote(src, dst, ssem, rsem, dev):
        return pltpu.make_async_remote_copy(src_ref=src, dst_ref=dst, send_sem=ssem, recv_sem=rsem, device_id={"ep": dev}, device_id_type=MESH_ID)

    small = []
    for i, d in enumerate(peers):
        for k, ref in enumerate((gv_all, tk_all, sl_all, pc_all)):
            c = remote(ref.at[me], ref.at[me], ss_sem.at[i, k], sr_sem.at[i, k], d)
            c.start()
            small.append(c)
    to_far = []
    for h in range(2):
        rows = pl.ds(h * half, half)
        c = remote(gy_all.at[me, rows], gy_all.at[me, rows], gs_sem.at[1 + h], gr_sem.at[1 + h], far)
        c.start()
        to_far.append(c)
    to_partner = remote(gy_all.at[me], gy_all.at[me], gs_sem.at[0], gr_sem.at[0], partner)
    to_partner.start()

    def build(s):
        ids = tk_all[s]
        slots = sl_all[s]
        gates = gv_all[s]
        counts = pc_all[s]
        lane = lax.broadcasted_iota(jnp.int32, counts.shape, 1)
        row_c = lax.broadcasted_iota(jnp.int32, (cap, tok), 0).astype(F32)
        hots, cols = [], []
        for e in range(n_loc):
            g = me * n_loc + e
            cnt = jnp.sum(jnp.where(lane == g, counts.astype(F32), 0.0), axis=1, keepdims=True)
            slots_f = slots.astype(F32)
            ok = (ids == g) & (slots >= 0) & (slots_f < cnt)
            slot_row = jnp.max(jnp.where(ok, slots_f, -1.0), axis=0, keepdims=True)
            gate_row = jnp.sum(jnp.where(ok, gates, 0.0), axis=0, keepdims=True)
            hit = row_c == slot_row
            cols.append(jnp.sum(jnp.where(hit, gate_row, 0.0), axis=1, keepdims=True))
            hots.append(jnp.where(hit, 1.0, 0.0).astype(BF16))
        hot = jnp.concatenate(hots, axis=0)
        p_all[s] = hot
        for n in range(0, dim, 256):
            picked = jnp.dot(hot, gy_all[s, :, n:n + 256], preferred_element_type=F32)
            for e in range(n_loc):
                dd[e, s, :, n:n + 256] = (picked[e * cap:(e + 1) * cap] * cols[e]).astype(BF16)

    build(me)

    bulk[0].wait()
    bulk[1].wait()

    def pre(e, carry):
        h1 = hg_v[e].astype(F32)
        h3 = hu_v[e].astype(F32)
        sig = jax.nn.sigmoid(h1)
        act = h1 * sig
        aa[e] = (act * h3).astype(BF16)
        c1_v[e] = h3 * sig * (1.0 + h1 * (1.0 - sig))
        s_v[e] = act
        return carry

    lax.fori_loop(0, n_loc, pre, 0)

    bulk[2].wait()
    top_k = yr.shape[1]
    dots = lax.dot_general(yr_v[...].reshape(tok * top_k, dim), gy_all[me], NT, preferred_element_type=F32).reshape(tok, top_k, tok)
    same = lax.broadcasted_iota(jnp.int32, dots.shape, 0) == lax.broadcasted_iota(jnp.int32, dots.shape, 2)
    gg[...] = jnp.sum(jnp.where(same, dots, 0.0), axis=0)

    for k in range(4):
        small[k].wait_recv()
    to_partner.wait_recv()
    build(partner)

    relay = []
    for h in range(2):
        rows = pl.ds(h * half, half)
        to_far[h].wait_recv()
        c = remote(gy_all.at[far, rows], gy_all.at[far, rows], gs_sem.at[3 + h], gr_sem.at[3 + h], partner)
        c.start()
        relay.append(c)
    for k in range(4):
        small[4 + k].wait_recv()
    build(far)
    for k in range(4):
        small[8 + k].wait_recv()
    for h in range(2):
        relay[h].wait_recv()
    build(far_partner)

    def expert(e, carry):
        pltpu.make_async_copy(wd.at[e], wd_v.at[e], wd_sem.at[e]).wait()
        d_e = dd[e].reshape(4 * cap, dim)
        da = lax.dot_general(d_e, wd_v[e], NT, preferred_element_type=F32).astype(BF16).astype(F32)
        dh1 = (da * c1_v[e]).astype(BF16)
        dh3 = (da * s_v[e]).astype(BF16)
        dh[e, :, :ffn] = dh1
        dh[e, :, ffn:] = dh3
        pltpu.make_async_copy(wg.at[e], wg_v.at[e], wg_sem.at[e]).wait()
        pltpu.make_async_copy(wu.at[e], wu_v.at[e], wu_sem.at[e]).wait()
        for n in range(0, dim, 256):
            r = lax.dot_general(dh1, wg_v[e, n:n + 256], NT, preferred_element_type=F32) + lax.dot_general(dh3, wu_v[e, n:n + 256], NT, preferred_element_type=F32)
            r = r.astype(BF16)
            for s in range(4):
                r_all[s, e, :, n:n + 256] = r[s * cap:(s + 1) * cap]
        return carry

    lax.fori_loop(0, n_loc, expert, 0)

    for i, s in enumerate((me,) + peers):
        part[i] = lax.dot_general(p_all[s], r_all[s].reshape(n_loc * cap, dim), TN, preferred_element_type=F32)

    for c in small + to_far + [to_partner] + relay:
        c.wait_send()


def weight_kernel(x, dd, aa, dh, gg, owg, owu, owd, ogg, x_v, buf_d, buf_g, buf_u, in_sem, out_sem):
    n_loc = x.shape[0]
    ffn = aa.shape[2]
    pltpu.make_async_copy(x, x_v, in_sem).start()
    ogg[...] = gg[...]

    def out_copies(e, slot):
        return (pltpu.make_async_copy(buf_d.at[slot], owd.at[e], out_sem.at[slot, 0]),
                pltpu.make_async_copy(buf_g.at[slot], owg.at[e], out_sem.at[slot, 1]),
                pltpu.make_async_copy(buf_u.at[slot], owu.at[e], out_sem.at[slot, 2]))

    def expert(e, carry):
        slot = lax.rem(e, 2)
        c_d, c_g, c_u = out_copies(e, slot)

        @pl.when(e >= 2)
        def _():
            for c in out_copies(e - 2, slot):
                c.wait()
        buf_d[slot] = lax.dot_general(aa[e], dd[e], TN, preferred_element_type=F32)
        c_d.start()

        @pl.when(e == 0)
        def _():
            pltpu.make_async_copy(x, x_v, in_sem).wait()
        buf_g[slot] = lax.dot_general(x_v[e], dh[e, :, :ffn], TN, preferred_element_type=F32)
        c_g.start()
        buf_u[slot] = lax.dot_general(x_v[e], dh[e, :, ffn:], TN, preferred_element_type=F32)
        c_u.start()
        return carry

    lax.fori_loop(0, n_loc, expert, 0)
    for e in (n_loc - 2, n_loc - 1):
        for c in out_copies(e, e % 2):
            c.wait()


def solution(mesh):
    rows_spec = P(("dp", "ep"), None)
    cube_spec = P(("dp", "ep"), None, None)
    weight_spec = P("ep", None, None)

    def local_step(grad_y, gate_vals, topk_idx, slot_ids, pair_counts, y_routed, x_disp, h_gate, h_up, w_gate, w_up, w_down):
        tok, dim = grad_y.shape
        top_k = topk_idx.shape[1]
        n_loc, _, ffn = w_gate.shape
        rows = x_disp.shape[1]
        cap = rows // 4
        n_exp = pair_counts.shape[1]
        any_spec = pl.BlockSpec(memory_space=pl.ANY)
        vmem_spec = pl.BlockSpec(memory_space=pltpu.VMEM)
        dma = pltpu.SemaphoreType.DMA
        part, dd, aa, dh, gg = pl.pallas_call(
            token_kernel,
            out_shape=(jax.ShapeDtypeStruct((4, tok, dim), F32),
                       jax.ShapeDtypeStruct((n_loc, 4, cap, dim), BF16),
                       jax.ShapeDtypeStruct((n_loc, rows, ffn), BF16),
                       jax.ShapeDtypeStruct((n_loc, rows, 2 * ffn), BF16),
                       jax.ShapeDtypeStruct((top_k, tok), F32)),
            in_specs=[any_spec] * 11,
            out_specs=(vmem_spec,) * 5,
            scratch_shapes=[
                pltpu.VMEM((4, tok, dim), BF16), pltpu.VMEM((4, top_k, tok), F32), pltpu.VMEM((4, top_k, tok), jnp.int32), pltpu.VMEM((4, top_k, tok), jnp.int32), pltpu.VMEM((4, 1, n_exp), jnp.int32),
                pltpu.VMEM((tok, top_k, dim), BF16), pltpu.VMEM((n_loc, rows, ffn), BF16), pltpu.VMEM((n_loc, rows, ffn), BF16),
                pltpu.VMEM((n_loc, dim, ffn), BF16), pltpu.VMEM((n_loc, dim, ffn), BF16), pltpu.VMEM((n_loc, ffn, dim), BF16),
                pltpu.VMEM((n_loc, rows, ffn), F32), pltpu.VMEM((n_loc, rows, ffn), F32),
                pltpu.VMEM((4, n_loc * cap, tok), BF16), pltpu.VMEM((4, n_loc, cap, dim), BF16),
                dma((5,)), dma((3,)), dma((n_loc,)), dma((n_loc,)), dma((n_loc,)),
                dma((5,)), dma((5,)), dma((3, 4)), dma((3, 4)),
            ],
            compiler_params=pltpu.CompilerParams(collective_id=0, has_side_effects=True, vmem_limit_bytes=56 * 1024 * 1024),
            cost_estimate=pl.CostEstimate(flops=4_000_000_000, bytes_accessed=30_000_000, transcendentals=0),
            name="token_kernel",
        )(grad_y, gate_vals.T, topk_idx.T, slot_ids.T, pair_counts, y_routed, h_gate, h_up, w_gate, w_up, w_down)

        pairs = ([(i, i ^ 1) for i in range(4)], [(i, i ^ 2) for i in range(4)], [(i, i ^ 3) for i in range(4)])
        got = [lax.ppermute(part[i + 1], "ep", pairs[i]) for i in (2, 1, 0)]

        owg, owu, owd, ogg = pl.pallas_call(
            weight_kernel,
            out_shape=(jax.ShapeDtypeStruct((n_loc, dim, ffn), F32),
                       jax.ShapeDtypeStruct((n_loc, dim, ffn), F32),
                       jax.ShapeDtypeStruct((n_loc, ffn, dim), F32),
                       jax.ShapeDtypeStruct((top_k, tok), F32)),
            in_specs=[any_spec] + [vmem_spec] * 4,
            out_specs=(any_spec, any_spec, any_spec, vmem_spec),
            scratch_shapes=[pltpu.VMEM((n_loc, rows, dim), BF16), pltpu.VMEM((2, ffn, dim), F32), pltpu.VMEM((2, dim, ffn), F32), pltpu.VMEM((2, dim, ffn), F32), dma(()), dma((2, 3))],
            compiler_params=pltpu.CompilerParams(vmem_limit_bytes=32 * 1024 * 1024),
            cost_estimate=pl.CostEstimate(flops=16_000_000_000, bytes_accessed=56_000_000, transcendentals=0),
            name="weight_kernel",
        )(x_disp, dd.reshape(n_loc, rows, dim), aa, dh, gg)
        grad_x = (part[0] + got[2] + got[1] + got[0]).astype(BF16)
        return grad_x, ogg.T, owg, owu, owd

    return jax.shard_map(local_step, mesh=mesh, in_specs=(rows_spec, rows_spec, rows_spec, rows_spec, rows_spec, cube_spec, cube_spec, cube_spec, cube_spec, weight_spec, weight_spec, weight_spec), out_specs=(rows_spec, rows_spec, cube_spec, cube_spec, cube_spec), check_vma=False)
```

time: 158 us -> 55.6 us (0.35)
  local copies, waits for them, and re-layouts: 60.2 us -> 6.27 us
  matrix products: 52.5 us -> 0 us
  Pallas kernels: 0 us -> 43.6 us
  waiting for transfers between devices: 22.3 us -> 0.01 us
  starting transfers between devices: 13.7 us -> 3.01 us
  other arithmetic: 6.9 us -> 1.68 us
    dot_general x7 -> x0, matrix products: 52.5 us -> none  [the longest x1 10.5 us: expert_grads(): jnp.einsum('erf,erd->efd', hidden_act, grad_rows, preferred_element_type=...]
    pallas_call x0 -> x2, Pallas kernels: none -> 43.6 us  [the longest x1 26.5 us: local_step(): pl.pallas_call(token_kernel, out_shape=(jax.ShapeDtypeStruct((4, tok, dim...]
    unnamed x20 -> x10, local copies, waits for them, and re-layouts: 35.5 us -> 5.09 us
    all_to_all x3 -> x0, waiting for transfers between devices: 22.3 us -> none  [the longest x1 22.3 us: local_step(): lax.all_to_all(send_rows.reshape(n_dev, n_loc, cap_rows, model_dim), 'ep'...]
    gather x3 -> x0, local copies, waits for them, and re-layouts: 16.8 us -> none  [the longest x1 6.87 us: build_send(): jnp.take(gate_vals.reshape(-1), row_source, mode='fill', fill_value=0)]
    all_to_all x3 -> x0, starting transfers between devices: 13.7 us -> none  [the longest x1 4.62 us: local_step(): lax.all_to_all(grad_disp.reshape(n_loc, n_dev, cap_rows, model_dim), 'ep'...]
    ppermute x0 -> x3, starting transfers between devices: none -> 3.01 us  [local_step(): got = [lax.ppermute(part[i + 1], 'ep', pairs[i]) for i in (2, 1, 0)]]
    scatter x1 -> x0, local copies, waits for them, and re-layouts: 2.45 us -> none  [build_send(): jnp.full((n_exp * cap_rows,), tok_dev * top_k, jnp.int32).at[dest_row]]
  transfers between devices with their start and end apart: 3 -> 3, of which waited for: 1 -> 0; matrix products, arithmetic and copies ran while one was open for 55% -> 0% of each run, Pallas kernels for 0% -> 31%
where the time goes in v1:
time: 55.6 us; the launch traced here: 55.3 us
  Pallas kernels  43.6 us (78%)
  local copies, waits for them, and re-layouts  6.27 us (11%)
  starting transfers between devices  3.01 us (5%)
  other arithmetic  1.68 us (3%)
  between operations  0.71 us (1%)
    pallas_call x1, Pallas kernels, local_step(): pl.pallas_call(token_kernel, out_shape=(jax.ShapeDtypeStruct((4, tok, dim...  26.5 us
    pallas_call x1, Pallas kernels, local_step(): pl.pallas_call(weight_kernel, out_shape=(jax.ShapeDtypeStruct((n_loc, dim...  17.2 us
    unnamed x10, local copies, waits for them, and re-layouts  5.09 us
    ppermute x3, starting transfers between devices, local_step(): got = [lax.ppermute(part[i + 1], 'ep', pairs[i]) for i in (2, 1, 0)]  3.01 us
    convert_element_type x1, other arithmetic, local_step(): grad_x = (part[0] + got[2] + got[1] + got[0]).astype(BF16)  1.68 us
    squeeze x1, local copies, waits for them, and re-layouts, local_step(): got = [lax.ppermute(part[i + 1], 'ep', pairs[i]) for i in (2, 1, 0)]  1.18 us
  transfers between devices with their start and end apart: 3, of which 0 were waited for; matrix products, arithmetic and copies ran while one was open for 0% of the time, Pallas kernels for 31%

profile of v1, /device:TPU:0, one launch (start us, length us, event | category | flops | bytes accessed | tf_op | source)
XLA Modules:
  0.0 55.3 jit_solution(16895551205710235087)
XLA Ops:
  0.6 0.0 copy-start
  0.6 26.5 %token_kernel.1 = (f32[4,64,1024]{2,1,0:T(8,128)}, bf16[8,4,32,1024]{3,2,1,0:T(8,128)(2,1)}, bf16[8,128,512]{2,1,0:T(8,128)(2,1)}, bf16[8,128,1024]{2,1,0:T(8,128)(2,1)}, f32[8,64]{1,0:T(8,128)}) custom-call(bf16[64,1024]{1,0:T(8,128)(2,1)} %gy.1, f32[8,64]{1,0:T(8,128)} %bitcast.20, s32[8,64]{1,0:T(8,128)} %bitcast.21, s32[8,64]{1,0:T(8,128)} %bitcast.22, ...), custom_call_target="tpu_custom_call" | custom-call | flops 4000000000 | bytes 30000000 | tf_op jit(solution)/shard_map/token_kernel/pallas_call | solution.py:221
  27.1 1.2 %slice_bitcast_fusion.2 = (f32[64,1024]{1,0:T(8,128)S(1)}, f32[64,1024]{1,0:T(8,128)S(1)}, f32[64,1024]{1,0:T(8,128)S(1)}) fusion(f32[4,64,1024]{2,1,0:T(8,128)} %get-tuple-element.14), kind=kLoop, calls=%fused_computation.6 | loop fusion | bytes 1572864 | tf_op jit(solution)/shard_map/squeeze | solution.py:245
  28.3 0.0 collective-permute-start
  28.3 2.6 %collective-permute-start.2 = (f32[64,1024]{1,0:T(8,128)S(1)}, f32[64,1024]{1,0:T(8,128)S(1)}, u32[]{:S(2)}, u32[]{:S(2)}) collective-permute-start(f32[64,1024]{1,0:T(8,128)S(1)} %get-tuple-element.24), channel_id=1, source_target_pairs={{0,3},{1,2},{2,1},{3,0},{4,7},{5,6},{6,5},{7,4}} | collective-permute-start | bytes 786440 | tf_op jit(solution)/shard_map/ppermute | solution.py:245
  31.0 0.4 collective-permute-start.1
  31.3 0.0 copy-done
  31.3 0.0 copy-start.1
  31.3 1.6 %copy-done.1 = bf16[8,4,32,1024]{3,2,1,0:T(8,128)(2,1)S(1)} copy-done((bf16[8,4,32,1024]{3,2,1,0:T(8,128)(2,1)S(1)}, bf16[8,4,32,1024]{3,2,1,0:T(8,128)(2,1)}, u32[]{:S(2)}) %copy-start.1) | copy-done | bytes 2097176
  32.9 0.0 copy-start.2
  32.9 1.6 %copy-done.2 = bf16[8,128,1024]{2,1,0:T(8,128)(2,1)S(1)} copy-done((bf16[8,128,1024]{2,1,0:T(8,128)(2,1)S(1)}, bf16[8,128,1024]{2,1,0:T(8,128)(2,1)}, u32[]{:S(2)}) %copy-start.2) | copy-done | bytes 2097176
  34.5 0.0 copy-start.3
  34.5 1.2 %copy-done.3 = bf16[8,128,512]{2,1,0:T(8,128)(2,1)S(1)} copy-done((bf16[8,128,512]{2,1,0:T(8,128)(2,1)S(1)}, bf16[8,128,512]{2,1,0:T(8,128)(2,1)}, u32[]{:S(2)}) %copy-start.3) | copy-done | bytes 1048600
  35.7 0.0 copy-start.4
  35.7 0.7 %copy-done.4 = f32[8,64]{1,0:T(8,128)S(1)} copy-done((f32[8,64]{1,0:T(8,128)S(1)}, f32[8,64]{1,0:T(8,128)}, u32[]{:S(2)}) %copy-start.4) | copy-done | bytes 2072
  36.4 17.2 %weight_kernel.1 = (f32[8,1024,512]{2,1,0:T(8,128)}, f32[8,1024,512]{2,1,0:T(8,128)}, f32[8,512,1024]{2,1,0:T(8,128)}, f32[8,64]{1,0:T(8,128)}) custom-call(bf16[8,128,1024]{2,1,0:T(8,128)(2,1)S(1)} %copy-done, bf16[8,128,1024]{2,1,0:T(8,128)(2,1)S(1)} %bitcast.19, bf16[8,128,512]{2,1,0:T(8,128)(2,1)S(1)} %copy-done.3, bf16[8,128,1024]{2,1,0:T(8,128)(2,1)S(1)} %copy-done.2, ...), custom_call_target="tpu_custom_call" | custom-call | flops 16000000000 | bytes 56000000 | tf_op jit(solution)/shard_map/weight_kernel/pallas_call | solution.py:247
  53.6 0.0 collective-permute-done
  53.6 0.0 collective-permute-done.2
  53.6 0.0 collective-permute-done.1
  53.6 1.7 %fusion.2 = bf16[64,1024]{1,0:T(8,128)(2,1)} fusion(f32[64,1024]{1,0:T(8,128)S(1)} %collective-permute-done.2, f32[64,1024]{1,0:T(8,128)S(1)} %collective-permute-done.1, f32[64,1024]{1,0:T(8,128)S(1)} %collective-permute-done, f32[4,64,1024]{2,1,0:T(8,128)} %get-tuple-element.14), kind=kLoop, calls=%fused_computation.3 | loop fusion | flops 262144 | bytes 1179648 | tf_op jit(solution)/shard_map/convert_element_type | solution.py:260
Async XLA Ops:
  0.6 30.7 %copy-start = (bf16[8,128,1024]{2,1,0:T(8,128)(2,1)S(1)}, bf16[8,128,1024]{2,1,0:T(8,128)(2,1)}, u32[]{:S(2)}) copy-start(bf16[8,128,1024]{2,1,0:T(8,128)(2,1)} %x.1) | copy-start | bytes 6291460
  28.3 25.3 %collective-permute-start = (f32[64,1024]{1,0:T(8,128)S(1)}, f32[64,1024]{1,0:T(8,128)S(1)}, u32[]{:S(2)}, u32[]{:S(2)}) collective-permute-start(f32[64,1024]{1,0:T(8,128)S(1)} %get-tuple-element.23), channel_id=1, source_target_pairs={{0,1},{1,0},{2,3},{3,2},{4,5},{5,4},{6,7},{7,6}} | collective-permute-start | bytes 786440 | tf_op jit(solution)/shard_map/ppermute | solution.py:245
  28.3 25.3 %collective-permute-start.2 = (f32[64,1024]{1,0:T(8,128)S(1)}, f32[64,1024]{1,0:T(8,128)S(1)}, u32[]{:S(2)}, u32[]{:S(2)}) collective-permute-start(f32[64,1024]{1,0:T(8,128)S(1)} %get-tuple-element.24), channel_id=1, source_target_pairs={{0,3},{1,2},{2,1},{3,0},{4,7},{5,6},{6,5},{7,4}} | collective-permute-start | bytes 786440 | tf_op jit(solution)/shard_map/ppermute | solution.py:245
  31.0 22.7 %collective-permute-start.1 = (f32[64,1024]{1,0:T(8,128)S(1)}, f32[64,1024]{1,0:T(8,128)S(1)}, u32[]{:S(2)}, u32[]{:S(2)}) collective-permute-start(f32[64,1024]{1,0:T(8,128)S(1)} %get-tuple-element.25), channel_id=1, source_target_pairs={{0,2},{1,3},{2,0},{3,1},{4,6},{5,7},{6,4},{7,5}} | collective-permute-start | bytes 786440 | tf_op jit(solution)/shard_map/ppermute | solution.py:245
  31.3 1.6 %copy-start.1 = (bf16[8,4,32,1024]{3,2,1,0:T(8,128)(2,1)S(1)}, bf16[8,4,32,1024]{3,2,1,0:T(8,128)(2,1)}, u32[]{:S(2)}) copy-start(bf16[8,4,32,1024]{3,2,1,0:T(8,128)(2,1)} %get-tuple-element.15) | copy-start | bytes 6291460
  32.9 1.6 %copy-start.2 = (bf16[8,128,1024]{2,1,0:T(8,128)(2,1)S(1)}, bf16[8,128,1024]{2,1,0:T(8,128)(2,1)}, u32[]{:S(2)}) copy-start(bf16[8,128,1024]{2,1,0:T(8,128)(2,1)} %get-tuple-element.17.dh) | copy-start | bytes 6291460
  34.5 1.2 %copy-start.3 = (bf16[8,128,512]{2,1,0:T(8,128)(2,1)S(1)}, bf16[8,128,512]{2,1,0:T(8,128)(2,1)}, u32[]{:S(2)}) copy-start(bf16[8,128,512]{2,1,0:T(8,128)(2,1)} %get-tuple-element.16.aa) | copy-start | bytes 3145732
  35.7 0.7 %copy-start.4 = (f32[8,64]{1,0:T(8,128)S(1)}, f32[8,64]{1,0:T(8,128)}, u32[]{:S(2)}) copy-start(f32[8,64]{1,0:T(8,128)} %get-tuple-element.18.gg) | copy-start | bytes 6148

commit v2 on v1

v2 whole, which is shorter than its diff:
```python
import jax
import jax.numpy as jnp
from jax import lax
from jax.experimental import pallas as pl
from jax.experimental.pallas import tpu as pltpu
from jax.sharding import PartitionSpec as P

MESH_ID = pl.DeviceIdType.MESH
F32 = jnp.float32
BF16 = jnp.bfloat16
NT = (((1,), (1,)), ((), ()))
TN = (((0,), (0,)), ((), ()))
MIB = 1024 * 1024
COLS = 256


def peer_ids():
    me = lax.axis_index("ep")
    partner = me + 1 - 2 * lax.rem(me, 2)
    return me, partner, lax.rem(me + 2, 4), lax.rem(partner + 2, 4)


def comm_kernel(gy, gv, tk, sl, pc, yr, hg, hu, wg, wu, wd,
                dd, aa, c1, act_o, p_all, wg_v, wu_v, wd_v, gg,
                gy_all, gv_all, tk_all, sl_all, pc_all, yr_v, hg_v, hu_v,
                own_sem, bulk_sem, gs_sem, gr_sem, ss_sem, sr_sem):
    n_loc = wd.shape[0]
    cap = dd.shape[2]
    tok, dim = gy.shape
    half = tok // 2
    me, partner, far, far_partner = peer_ids()
    peers = (partner, far, far_partner)

    own = [pltpu.make_async_copy(gy, gy_all.at[me], own_sem.at[0]),
           pltpu.make_async_copy(gv, gv_all.at[me], own_sem.at[1]),
           pltpu.make_async_copy(tk, tk_all.at[me], own_sem.at[2]),
           pltpu.make_async_copy(sl, sl_all.at[me], own_sem.at[3]),
           pltpu.make_async_copy(pc, pc_all.at[me], own_sem.at[4])]
    for c in own:
        c.start()
    barrier = pltpu.get_barrier_semaphore()
    for d in peers:
        pl.semaphore_signal(barrier, inc=1, device_id={"ep": d}, device_id_type=MESH_ID)
    bulk = [pltpu.make_async_copy(src, dst, bulk_sem.at[i]) for i, (src, dst) in enumerate(((hg, hg_v), (hu, hu_v), (yr, yr_v), (wd, wd_v), (wg, wg_v), (wu, wu_v)))]
    for c in bulk:
        c.start(priority=1)
    for c in own:
        c.wait()
    pl.semaphore_wait(barrier, 3)

    def remote(src, dst, ssem, rsem, dev):
        return pltpu.make_async_remote_copy(src_ref=src, dst_ref=dst, send_sem=ssem, recv_sem=rsem, device_id={"ep": dev}, device_id_type=MESH_ID)

    small = []
    for i, d in enumerate(peers):
        for k, ref in enumerate((gv_all, tk_all, sl_all, pc_all)):
            c = remote(ref.at[me], ref.at[me], ss_sem.at[i, k], sr_sem.at[i, k], d)
            c.start()
            small.append(c)
    to_far = []
    for h in range(2):
        rows = pl.ds(h * half, half)
        c = remote(gy_all.at[me, rows], gy_all.at[me, rows], gs_sem.at[1 + h], gr_sem.at[1 + h], far)
        c.start()
        to_far.append(c)
    to_partner = remote(gy_all.at[me], gy_all.at[me], gs_sem.at[0], gr_sem.at[0], partner)
    to_partner.start()

    def build(s):
        ids = tk_all[s]
        slots = sl_all[s]
        gates = gv_all[s]
        counts = pc_all[s]
        lane = lax.broadcasted_iota(jnp.int32, counts.shape, 1)
        row_c = lax.broadcasted_iota(jnp.int32, (cap, tok), 0).astype(F32)
        hots, cols = [], []
        for e in range(n_loc):
            g = me * n_loc + e
            cnt = jnp.sum(jnp.where(lane == g, counts.astype(F32), 0.0), axis=1, keepdims=True)
            slots_f = slots.astype(F32)
            ok = (ids == g) & (slots >= 0) & (slots_f < cnt)
            slot_row = jnp.max(jnp.where(ok, slots_f, -1.0), axis=0, keepdims=True)
            gate_row = jnp.sum(jnp.where(ok, gates, 0.0), axis=0, keepdims=True)
            hit = row_c == slot_row
            cols.append(jnp.sum(jnp.where(hit, gate_row, 0.0), axis=1, keepdims=True))
            hots.append(jnp.where(hit, 1.0, 0.0).astype(BF16))
        hot = jnp.concatenate(hots, axis=0)
        p_all[s] = hot
        for n in range(0, dim, COLS):
            picked = jnp.dot(hot, gy_all[s, :, n:n + COLS], preferred_element_type=F32)
            for e in range(n_loc):
                dd[e, s, :, n:n + COLS] = (picked[e * cap:(e + 1) * cap] * cols[e]).astype(BF16)

    build(me)

    bulk[0].wait()
    bulk[1].wait()

    def pre(e, carry):
        h1 = hg_v[e].astype(F32)
        h3 = hu_v[e].astype(F32)
        sig = jax.nn.sigmoid(h1)
        act = h1 * sig
        aa[e] = (act * h3).astype(BF16)
        c1[e] = h3 * sig * (1.0 + h1 * (1.0 - sig))
        act_o[e] = act
        return carry

    lax.fori_loop(0, n_loc, pre, 0)

    bulk[2].wait()
    top_k = yr.shape[1]
    dots = lax.dot_general(yr_v[...].reshape(tok * top_k, dim), gy_all[me], NT, preferred_element_type=F32).reshape(tok, top_k, tok)
    same = lax.broadcasted_iota(jnp.int32, dots.shape, 0) == lax.broadcasted_iota(jnp.int32, dots.shape, 2)
    gg[...] = jnp.sum(jnp.where(same, dots, 0.0), axis=0)

    for k in range(4):
        small[k].wait_recv()
    to_partner.wait_recv()
    build(partner)

    relay = []
    for h in range(2):
        rows = pl.ds(h * half, half)
        to_far[h].wait_recv()
        c = remote(gy_all.at[far, rows], gy_all.at[far, rows], gs_sem.at[3 + h], gr_sem.at[3 + h], partner)
        c.start()
        relay.append(c)
    for k in range(4):
        small[4 + k].wait_recv()
    build(far)
    for k in range(4):
        small[8 + k].wait_recv()
    for h in range(2):
        relay[h].wait_recv()
    build(far_partner)

    for c in bulk[3:]:
        c.wait()
    for c in small + to_far + [to_partner] + relay:
        c.wait_send()


def chain_kernel(dd, aa, c1, act, p_all, wg, wu, wd, p_own, p_partner, p_far, p_far_partner, dh, owd, r_all, buf_d, out_sem):
    n_loc, _, cap, dim = dd.shape
    ffn = aa.shape[2]
    outs = []

    def first(e):
        d_e = dd[e].reshape(4 * cap, dim)
        for n in range(0, ffn, COLS):
            da = lax.dot_general(d_e, wd[e, n:n + COLS], NT, preferred_element_type=F32).astype(BF16).astype(F32)
            dh[e, :, n:n + COLS] = (da * c1[e, :, n:n + COLS]).astype(BF16)
            dh[e, :, ffn + n:ffn + n + COLS] = (da * act[e, :, n:n + COLS]).astype(BF16)

    def second(e):
        dh1 = dh[e, :, :ffn]
        dh3 = dh[e, :, ffn:]
        for n in range(0, dim, COLS):
            r = lax.dot_general(dh1, wg[e, n:n + COLS], NT, preferred_element_type=F32) + lax.dot_general(dh3, wu[e, n:n + COLS], NT, preferred_element_type=F32)
            r = r.astype(BF16)
            for s in range(4):
                r_all[s, e, :, n:n + COLS] = r[s * cap:(s + 1) * cap]

    def down(e):
        slot = e % 2
        if e >= 2:
            outs[e - 2].wait()
        buf_d[slot] = lax.dot_general(aa[e], dd[e].reshape(4 * cap, dim), TN, preferred_element_type=F32)
        c = pltpu.make_async_copy(buf_d.at[slot], owd.at[e], out_sem.at[slot])
        c.start()
        outs.append(c)

    for e in range(n_loc):
        first(e)
        down(e)
        if e >= 1:
            second(e - 1)
    second(n_loc - 1)

    me, partner, far, far_partner = peer_ids()
    for s, ref in ((me, p_own), (partner, p_partner), (far, p_far), (far_partner, p_far_partner)):
        ref[...] = lax.dot_general(p_all[s], r_all[s].reshape(n_loc * cap, dim), TN, preferred_element_type=F32)
    for c in outs[-2:]:
        c.wait()


def weight_kernel(x, dh, gg, owg, owu, ogg, buf_g, buf_u, out_sem):
    n_loc = x.shape[0]
    ffn = owg.shape[2]
    ogg[...] = gg[...]

    def out_copies(e, slot):
        return (pltpu.make_async_copy(buf_g.at[slot], owg.at[e], out_sem.at[slot, 0]),
                pltpu.make_async_copy(buf_u.at[slot], owu.at[e], out_sem.at[slot, 1]))

    def expert(e, carry):
        slot = lax.rem(e, 2)
        c_g, c_u = out_copies(e, slot)

        @pl.when(e >= 2)
        def _():
            for c in out_copies(e - 2, slot):
                c.wait()
        buf_g[slot] = lax.dot_general(x[e], dh[e, :, :ffn], TN, preferred_element_type=F32)
        c_g.start()
        buf_u[slot] = lax.dot_general(x[e], dh[e, :, ffn:], TN, preferred_element_type=F32)
        c_u.start()
        return carry

    lax.fori_loop(0, n_loc, expert, 0)
    for e in (n_loc - 2, n_loc - 1):
        for c in out_copies(e, e % 2):
            c.wait()


def solution(mesh):
    rows_spec = P(("dp", "ep"), None)
    cube_spec = P(("dp", "ep"), None, None)
    weight_spec = P("ep", None, None)

    def local_step(grad_y, gate_vals, topk_idx, slot_ids, pair_counts, y_routed, x_disp, h_gate, h_up, w_gate, w_up, w_down):
        tok, dim = grad_y.shape
        top_k = topk_idx.shape[1]
        n_loc, _, ffn = w_gate.shape
        rows = x_disp.shape[1]
        cap = rows // 4
        n_exp = pair_counts.shape[1]
        hbm_spec = pl.BlockSpec(memory_space=pltpu.HBM)
        any_spec = pl.BlockSpec(memory_space=pl.ANY)
        vmem_spec = pl.BlockSpec(memory_space=pltpu.VMEM)
        dma = pltpu.SemaphoreType.DMA
        shape = jax.ShapeDtypeStruct
        ins = [pltpu.with_memory_space_constraint(a, pltpu.HBM) for a in (grad_y, gate_vals.T, topk_idx.T, slot_ids.T, pair_counts, y_routed, h_gate, h_up, w_gate, w_up, w_down)]
        dd, aa, c1, act, p_all, wg_v, wu_v, wd_v, gg = pl.pallas_call(
            comm_kernel,
            out_shape=(shape((n_loc, 4, cap, dim), BF16), shape((n_loc, rows, ffn), BF16), shape((n_loc, rows, ffn), F32), shape((n_loc, rows, ffn), F32),
                       shape((4, n_loc * cap, tok), BF16), shape(w_gate.shape, BF16), shape(w_up.shape, BF16), shape(w_down.shape, BF16), shape((top_k, tok), F32)),
            in_specs=[hbm_spec] * 11,
            out_specs=(vmem_spec,) * 9,
            scratch_shapes=[
                pltpu.VMEM((4, tok, dim), BF16), pltpu.VMEM((4, top_k, tok), F32), pltpu.VMEM((4, top_k, tok), jnp.int32), pltpu.VMEM((4, top_k, tok), jnp.int32), pltpu.VMEM((4, 1, n_exp), jnp.int32),
                pltpu.VMEM((tok, top_k, dim), BF16), pltpu.VMEM((n_loc, rows, ffn), BF16), pltpu.VMEM((n_loc, rows, ffn), BF16),
                dma((5,)), dma((6,)), dma((5,)), dma((5,)), dma((3, 4)), dma((3, 4)),
            ],
            compiler_params=pltpu.CompilerParams(collective_id=0, has_side_effects=True, vmem_limit_bytes=8 * MIB),
            cost_estimate=pl.CostEstimate(flops=1_000_000_000, bytes_accessed=30_000_000, transcendentals=0),
            name="comm_kernel",
        )(*ins)

        p_own, p_partner, p_far, p_far_partner, dh, owd = pl.pallas_call(
            chain_kernel,
            out_shape=(shape((tok, dim), F32),) * 4 + (shape((n_loc, rows, 2 * ffn), BF16), shape((n_loc, ffn, dim), F32)),
            in_specs=[vmem_spec] * 8,
            out_specs=(vmem_spec,) * 5 + (hbm_spec,),
            scratch_shapes=[pltpu.VMEM((4, n_loc, cap, dim), BF16), pltpu.VMEM((2, ffn, dim), F32), dma((2,))],
            compiler_params=pltpu.CompilerParams(vmem_limit_bytes=12 * MIB),
            cost_estimate=pl.CostEstimate(flops=4_000_000_000, bytes_accessed=20_000_000, transcendentals=0),
            name="chain_kernel",
        )(dd, aa, c1, act, p_all, wg_v, wu_v, wd_v)

        pairs = [[(i, i ^ k) for i in range(4)] for k in (1, 2, 3)]
        got_fp = lax.ppermute(p_far_partner, "ep", pairs[2])
        got_f = lax.ppermute(p_far, "ep", pairs[1])
        got_p = lax.ppermute(p_partner, "ep", pairs[0])

        owg, owu, ogg = pl.pallas_call(
            weight_kernel,
            out_shape=(shape((n_loc, dim, ffn), F32), shape((n_loc, dim, ffn), F32), shape((top_k, tok), F32)),
            in_specs=[vmem_spec] * 3,
            out_specs=(hbm_spec, hbm_spec, vmem_spec),
            scratch_shapes=[pltpu.VMEM((2, dim, ffn), F32), pltpu.VMEM((2, dim, ffn), F32), dma((2, 2))],
            compiler_params=pltpu.CompilerParams(vmem_limit_bytes=16 * MIB),
            cost_estimate=pl.CostEstimate(flops=16_000_000_000, bytes_accessed=56_000_000, transcendentals=0),
            name="weight_kernel",
        )(x_disp, dh, gg)
        grad_x = (p_own + got_p + got_f + got_fp).astype(BF16)
        return grad_x, ogg.T, owg, owu, owd

    return jax.shard_map(local_step, mesh=mesh, in_specs=(rows_spec, rows_spec, rows_spec, rows_spec, rows_spec, cube_spec, cube_spec, cube_spec, cube_spec, weight_spec, weight_spec, weight_spec), out_specs=(rows_spec, rows_spec, cube_spec, cube_spec, cube_spec), check_vma=False)
```

time: 55.6 us -> 39.2 us (0.71)
  Pallas kernels: 43.6 us -> 33.9 us
  local copies, waits for them, and re-layouts: 6.27 us -> 0.01 us
  other arithmetic: 1.68 us -> 0.71 us
    pallas_call x2 -> x3, Pallas kernels: 43.6 us -> 33.9 us  [the longest x1 12.3 us: local_step(): pl.pallas_call(chain_kernel, out_shape=(shape((tok, dim), F32),) * 4 + (s...]
    unnamed x10 -> x2, local copies, waits for them, and re-layouts: 5.09 us -> 0.01 us
    squeeze x1 -> x0, local copies, waits for them, and re-layouts: 1.18 us -> none  [local_step(): got = [lax.ppermute(part[i + 1], 'ep', pairs[i]) for i in (2, 1, 0)]]
    convert_element_type x1, other arithmetic: 1.68 us -> 0.71 us  [local_step(): grad_x = (p_own + got_p + got_f + got_fp).astype(BF16)]
  transfers between devices with their start and end apart: 3 -> 3, of which waited for: 0 -> 1; matrix products, arithmetic and copies ran while one was open for 0% -> 0% of each run, Pallas kernels for 31% -> 31%
where the time goes in v2:
time: 39.2 us; the launch traced here: 39.1 us
  Pallas kernels  33.9 us (86%)
  starting transfers between devices  3.48 us (9%)
  other arithmetic  0.71 us (2%)
  between operations  0.69 us (2%)
    pallas_call x1, Pallas kernels, local_step(): pl.pallas_call(chain_kernel, out_shape=(shape((tok, dim), F32),) * 4 + (s...  12.3 us
    pallas_call x1, Pallas kernels, local_step(): pl.pallas_call(weight_kernel, out_shape=(shape((n_loc, dim, ffn), F32), s...  12 us
    pallas_call x1, Pallas kernels, local_step(): pl.pallas_call(comm_kernel, out_shape=(shape((n_loc, 4, cap, dim), BF16),...  9.67 us
    ppermute x1, starting transfers between devices, local_step(): got_f = lax.ppermute(p_far, 'ep', pairs[1])  2.51 us
    ppermute x1, starting transfers between devices, local_step(): got_p = lax.ppermute(p_partner, 'ep', pairs[0])  0.88 us
  transfers between devices with their start and end apart: 3, of which 1 were waited for; matrix products, arithmetic and copies ran while one was open for 0% of the time, Pallas kernels for 31%

profile of v2, /device:TPU:0, one launch (start us, length us, event | category | flops | bytes accessed | tf_op | source)
XLA Modules:
  0.0 39.1 jit_solution(14302351358738778054)
XLA Ops:
  0.6 9.7 %comm_kernel.1 = (bf16[8,4,32,1024]{3,2,1,0:T(8,128)(2,1)S(1)}, bf16[8,128,512]{2,1,0:T(8,128)(2,1)S(1)}, f32[8,128,512]{2,1,0:T(8,128)S(1)}, f32[8,128,512]{2,1...) custom-call(bf16[64,1024]{1,0:T(8,128)(2,1)} %gy.1, ...), custom_call_target="tpu_custom_call" | custom-call | flops 1000000000 | bytes 30000000 | tf_op jit(solution)/shard_map/comm_kernel/pallas_call | solution.py:235
  10.3 0.0 copy-start
  10.3 12.3 %chain_kernel.1 = (f32[64,1024]{1,0:T(8,128)S(1)}, f32[64,1024]{1,0:T(8,128)S(1)}, f32[64,1024]{1,0:T(8,128)S(1)}, f32[64,1024]{1,0:T(8,128)S(1)}, bf16[8,128,10...) custom-call(bf16[8,4,32,1024]{3,2,1,0:T(8,128)(2,1)S(1)} %get-tuple-element.23.dd, ...), custom_call_target="tpu_custom_call" | custom-call | flops 4000000000 | bytes 20000000 | tf_op jit(solution)/shard_map/chain_kernel/pallas_call | solution.py:251
  22.6 0.9 %collective-permute-start = (f32[64,1024]{1,0:T(8,128)S(1)}, f32[64,1024]{1,0:T(8,128)S(1)}, u32[]{:S(2)}, u32[]{:S(2)}) collective-permute-start(f32[64,1024]{1,0:T(8,128)S(1)} %get-tuple-element.32), channel_id=1, source_target_pairs={{0,1},{1,0},{2,3},{3,2},{4,5},{5,4},{6,7},{7,6}} | collective-permute-start | bytes 786440 | tf_op jit(solution)/shard_map/ppermute | solution.py:265
  23.5 2.5 %collective-permute-start.1 = (f32[64,1024]{1,0:T(8,128)S(1)}, f32[64,1024]{1,0:T(8,128)S(1)}, u32[]{:S(2)}, u32[]{:S(2)}) collective-permute-start(f32[64,1024]{1,0:T(8,128)S(1)} %get-tuple-element.33), channel_id=1, source_target_pairs={{0,2},{1,3},{2,0},{3,1},{4,6},{5,7},{6,4},{7,5}} | collective-permute-start | bytes 786440 | tf_op jit(solution)/shard_map/ppermute | solution.py:264
  26.0 0.1 collective-permute-start.2
  26.1 0.0 copy-done
  26.1 12.0 %weight_kernel.1 = (f32[8,1024,512]{2,1,0:T(8,128)}, f32[8,1024,512]{2,1,0:T(8,128)}, f32[8,64]{1,0:T(8,128)}) custom-call(bf16[8,128,1024]{2,1,0:T(8,128)(2,1)S(1)} %copy-done, bf16[8,128,1024]{2,1,0:T(8,128)(2,1)S(1)} %get-tuple-element.35.dh, f32[8,64]{1,0:T(8,128)S(1)} %get-tuple-element.36.gg), custom_call_target="tpu_custom_call" | custom-call | flops 16000000000 | bytes 56000000 | tf_op jit(solution)/shard_map/weight_kernel/pallas_call | solution.py:267
  38.1 0.0 collective-permute-done
  38.1 0.0 collective-permute-done.1
  38.1 0.2 collective-permute-done.2
  38.4 0.7 %add_convert_fusion = bf16[64,1024]{1,0:T(8,128)(2,1)} fusion(f32[64,1024]{1,0:T(8,128)S(1)} %collective-permute-done.2, f32[64,1024]{1,0:T(8,128)S(1)} %collective-permute-done.1, f32[64,1024]{1,0:T(8,128)S(1)} %get-tuple-element.31, f32[64,1024]{1,0:T(8,128)S(1)} %collective-permute-done), kind=kLoop, calls=%fused_computation | loop fusion | flops 262144 | bytes 1179648 | tf_op jit(solution)/shard_map/convert_element_type | solution.py:277
Async XLA Ops:
  10.3 15.8 %copy-start = (bf16[8,128,1024]{2,1,0:T(8,128)(2,1)S(1)}, bf16[8,128,1024]{2,1,0:T(8,128)(2,1)}, u32[]{:S(2)}) copy-start(bf16[8,128,1024]{2,1,0:T(8,128)(2,1)} %x.1) | copy-start | bytes 6291460
  22.6 15.5 %collective-permute-start = (f32[64,1024]{1,0:T(8,128)S(1)}, f32[64,1024]{1,0:T(8,128)S(1)}, u32[]{:S(2)}, u32[]{:S(2)}) collective-permute-start(f32[64,1024]{1,0:T(8,128)S(1)} %get-tuple-element.32), channel_id=1, source_target_pairs={{0,1},{1,0},{2,3},{3,2},{4,5},{5,4},{6,7},{7,6}} | collective-permute-start | bytes 786440 | tf_op jit(solution)/shard_map/ppermute | solution.py:265
  23.5 14.6 %collective-permute-start.1 = (f32[64,1024]{1,0:T(8,128)S(1)}, f32[64,1024]{1,0:T(8,128)S(1)}, u32[]{:S(2)}, u32[]{:S(2)}) collective-permute-start(f32[64,1024]{1,0:T(8,128)S(1)} %get-tuple-element.33), channel_id=1, source_target_pairs={{0,2},{1,3},{2,0},{3,1},{4,6},{5,7},{6,4},{7,5}} | collective-permute-start | bytes 786440 | tf_op jit(solution)/shard_map/ppermute | solution.py:264
  26.0 12.3 %collective-permute-start.2 = (f32[64,1024]{1,0:T(8,128)S(1)}, f32[64,1024]{1,0:T(8,128)S(1)}, u32[]{:S(2)}, u32[]{:S(2)}) collective-permute-start(f32[64,1024]{1,0:T(8,128)S(1)} %get-tuple-element.34), channel_id=1, source_target_pairs={{0,3},{1,2},{2,1},{3,0},{4,7},{5,6},{6,5},{7,4}} | collective-permute-start | bytes 786440 | tf_op jit(solution)/shard_map/ppermute | solution.py:263

commit v3 on v2

--- a/solution.py
+++ b/solution.py
@@ -12,6 +12,7 @@
 TN = (((0,), (0,)), ((), ()))
 MIB = 1024 * 1024
 COLS = 256
+LATE = 2
 
 
 def peer_ids():
@@ -28,6 +29,7 @@
     cap = dd.shape[2]
     tok, dim = gy.shape
     half = tok // 2
+    early = wg_v.shape[0]
     me, partner, far, far_partner = peer_ids()
     peers = (partner, far, far_partner)
 
@@ -41,7 +43,7 @@
     barrier = pltpu.get_barrier_semaphore()
     for d in peers:
         pl.semaphore_signal(barrier, inc=1, device_id={"ep": d}, device_id_type=MESH_ID)
-    bulk = [pltpu.make_async_copy(src, dst, bulk_sem.at[i]) for i, (src, dst) in enumerate(((hg, hg_v), (hu, hu_v), (yr, yr_v), (wd, wd_v), (wg, wg_v), (wu, wu_v)))]
+    bulk = [pltpu.make_async_copy(src, dst, bulk_sem.at[i]) for i, (src, dst) in enumerate(((hg, hg_v), (hu, hu_v), (yr, yr_v), (wd, wd_v), (wg.at[pl.ds(0, early)], wg_v), (wu.at[pl.ds(0, early)], wu_v)))]
     for c in bulk:
         c.start(priority=1)
     for c in own:
@@ -52,19 +54,16 @@
         return pltpu.make_async_remote_copy(src_ref=src, dst_ref=dst, send_sem=ssem, recv_sem=rsem, device_id={"ep": dev}, device_id_type=MESH_ID)
 
     small = []
+    to_far = []
+    to_partner = remote(gy_all.at[me], gy_all.at[me], gs_sem.at[0], gr_sem.at[0], partner)
+    for h in range(2):
+        rows = pl.ds(h * half, half)
+        to_far.append(remote(gy_all.at[me, rows], gy_all.at[me, rows], gs_sem.at[1 + h], gr_sem.at[1 + h], far))
     for i, d in enumerate(peers):
         for k, ref in enumerate((gv_all, tk_all, sl_all, pc_all)):
-            c = remote(ref.at[me], ref.at[me], ss_sem.at[i, k], sr_sem.at[i, k], d)
-            c.start()
-            small.append(c)
-    to_far = []
-    for h in range(2):
-        rows = pl.ds(h * half, half)
-        c = remote(gy_all.at[me, rows], gy_all.at[me, rows], gs_sem.at[1 + h], gr_sem.at[1 + h], far)
-        c.start()
-        to_far.append(c)
-    to_partner = remote(gy_all.at[me], gy_all.at[me], gs_sem.at[0], gr_sem.at[0], partner)
-    to_partner.start()
+            small.append(remote(ref.at[me], ref.at[me], ss_sem.at[i, k], sr_sem.at[i, k], d))
+    for c in to_far + small + [to_partner]:
+        c.start()
 
     def build(s):
         ids = tk_all[s]
@@ -141,42 +140,62 @@
         c.wait_send()
 
 
-def chain_kernel(dd, aa, c1, act, p_all, wg, wu, wd, p_own, p_partner, p_far, p_far_partner, dh, owd, r_all, buf_d, out_sem):
+def mix(main, side):
+    done = 0
+    for k, work in enumerate(main):
+        work()
+        upto = len(side) * (k + 1) // len(main)
+        for extra in side[done:upto]:
+            extra()
+        done = upto
+
+
+def chain_kernel(dd, aa, c1, act, p_all, wg, wu, wd, wg_hbm, wu_hbm, p_own, p_partner, p_far, p_far_partner, dh, owd, r_all, buf_d, wg_l, wu_l, out_sem, in_sem):
     n_loc, _, cap, dim = dd.shape
     ffn = aa.shape[2]
-    outs = []
-
-    def first(e):
-        d_e = dd[e].reshape(4 * cap, dim)
-        for n in range(0, ffn, COLS):
-            da = lax.dot_general(d_e, wd[e, n:n + COLS], NT, preferred_element_type=F32).astype(BF16).astype(F32)
+    early = wg.shape[0]
+    pairs = n_loc // 2
+    ins = [pltpu.make_async_copy(wg_hbm.at[pl.ds(early, LATE)], wg_l, in_sem.at[0]), pltpu.make_async_copy(wu_hbm.at[pl.ds(early, LATE)], wu_l, in_sem.at[1])]
+    for c in ins:
+        c.start()
+
+    def first(e, n):
+        def work():
+            da = lax.dot_general(dd[e].reshape(4 * cap, dim), wd[e, n:n + COLS], NT, preferred_element_type=F32).astype(BF16).astype(F32)
             dh[e, :, n:n + COLS] = (da * c1[e, :, n:n + COLS]).astype(BF16)
             dh[e, :, ffn + n:ffn + n + COLS] = (da * act[e, :, n:n + COLS]).astype(BF16)
-
-    def second(e):
-        dh1 = dh[e, :, :ffn]
-        dh3 = dh[e, :, ffn:]
-        for n in range(0, dim, COLS):
-            r = lax.dot_general(dh1, wg[e, n:n + COLS], NT, preferred_element_type=F32) + lax.dot_general(dh3, wu[e, n:n + COLS], NT, preferred_element_type=F32)
+        return work
+
+    def second(e, n):
+        def work():
+            g, u = (wg[e, n:n + COLS], wu[e, n:n + COLS]) if e < early else (wg_l[e - early, n:n + COLS], wu_l[e - early, n:n + COLS])
+            r = lax.dot_general(dh[e, :, :ffn], g, NT, preferred_element_type=F32) + lax.dot_general(dh[e, :, ffn:], u, NT, preferred_element_type=F32)
             r = r.astype(BF16)
             for s in range(4):
                 r_all[s, e, :, n:n + COLS] = r[s * cap:(s + 1) * cap]
-
-    def down(e):
-        slot = e % 2
-        if e >= 2:
-            outs[e - 2].wait()
-        buf_d[slot] = lax.dot_general(aa[e], dd[e].reshape(4 * cap, dim), TN, preferred_element_type=F32)
-        c = pltpu.make_async_copy(buf_d.at[slot], owd.at[e], out_sem.at[slot])
-        c.start()
-        outs.append(c)
-
-    for e in range(n_loc):
-        first(e)
-        down(e)
-        if e >= 1:
-            second(e - 1)
-    second(n_loc - 1)
+        return work
+
+    def down(e, n, m):
+        def work():
+            buf_d[(e // 2) % 2, e % 2, m:m + COLS, n:n + COLS] = lax.dot_general(aa[e, :, m:m + COLS], dd[e, :, :, n:n + COLS].reshape(4 * cap, COLS), TN, preferred_element_type=F32)
+        return work
+
+    outs = [pltpu.make_async_copy(buf_d.at[p % 2], owd.at[pl.ds(2 * p, 2)], out_sem.at[p % 2]) for p in range(pairs)]
+    for p in range(-1, pairs):
+        main, side = [], []
+        if p >= 0:
+            main += [second(2 * p + i, n) for n in range(0, dim, COLS) for i in range(2)]
+        if p + 1 < pairs:
+            main += [first(2 * p + 2 + i, n) for n in range(0, ffn, COLS) for i in range(2)]
+            side += [down(2 * p + 2 + i, n, m) for i in range(2) for n in range(0, dim, COLS) for m in range(0, ffn, COLS)]
+            if p >= 1:
+                outs[p - 1].wait()
+        else:
+            for c in ins:
+                c.wait()
+        mix(main, side)
+        if p + 1 < pairs:
+            outs[p + 1].start()
 
     me, partner, far, far_partner = peer_ids()
     for s, ref in ((me, p_own), (partner, p_partner), (far, p_far), (far_partner, p_far_partner)):
@@ -235,7 +254,7 @@
         dd, aa, c1, act, p_all, wg_v, wu_v, wd_v, gg = pl.pallas_call(
             comm_kernel,
             out_shape=(shape((n_loc, 4, cap, dim), BF16), shape((n_loc, rows, ffn), BF16), shape((n_loc, rows, ffn), F32), shape((n_loc, rows, ffn), F32),
-                       shape((4, n_loc * cap, tok), BF16), shape(w_gate.shape, BF16), shape(w_up.shape, BF16), shape(w_down.shape, BF16), shape((top_k, tok), F32)),
+                       shape((4, n_loc * cap, tok), BF16), shape((n_loc - LATE, dim, ffn), BF16), shape((n_loc - LATE, dim, ffn), BF16), shape(w_down.shape, BF16), shape((top_k, tok), F32)),
             in_specs=[hbm_spec] * 11,
             out_specs=(vmem_spec,) * 9,
             scratch_shapes=[
@@ -251,13 +270,13 @@
         p_own, p_partner, p_far, p_far_partner, dh, owd = pl.pallas_call(
             chain_kernel,
             out_shape=(shape((tok, dim), F32),) * 4 + (shape((n_loc, rows, 2 * ffn), BF16), shape((n_loc, ffn, dim), F32)),
-            in_specs=[vmem_spec] * 8,
+            in_specs=[vmem_spec] * 8 + [hbm_spec] * 2,
             out_specs=(vmem_spec,) * 5 + (hbm_spec,),
-            scratch_shapes=[pltpu.VMEM((4, n_loc, cap, dim), BF16), pltpu.VMEM((2, ffn, dim), F32), dma((2,))],
-            compiler_params=pltpu.CompilerParams(vmem_limit_bytes=12 * MIB),
+            scratch_shapes=[pltpu.VMEM((4, n_loc, cap, dim), BF16), pltpu.VMEM((2, 2, ffn, dim), F32), pltpu.VMEM((LATE, dim, ffn), BF16), pltpu.VMEM((LATE, dim, ffn), BF16), dma((2,)), dma((2,))],
+            compiler_params=pltpu.CompilerParams(vmem_limit_bytes=18 * MIB),
             cost_estimate=pl.CostEstimate(flops=4_000_000_000, bytes_accessed=20_000_000, transcendentals=0),
             name="chain_kernel",
-        )(dd, aa, c1, act, p_all, wg_v, wu_v, wd_v)
+        )(dd, aa, c1, act, p_all, wg_v, wu_v, wd_v, ins[8], ins[9])
 
         pairs = [[(i, i ^ k) for i in range(4)] for k in (1, 2, 3)]
         got_fp = lax.ppermute(p_far_partner, "ep", pairs[2])

time: 39.2 us -> 35.4 us (0.903)
  Pallas kernels: 33.9 us -> 31.4 us
  starting transfers between devices: 3.48 us -> 2.47 us
    pallas_call x1, Pallas kernels: 12.3 us -> 9.97 us  [local_step(): pl.pallas_call(chain_kernel, out_shape=(shape((tok, dim), F32),) * 4 + (s...]
    ppermute x1, starting transfers between devices: 2.51 us -> 1.75 us  [local_step(): got_f = lax.ppermute(p_far, 'ep', pairs[1])]
  transfers between devices with their start and end apart: 3 -> 3, of which waited for: 1 -> 0; matrix products, arithmetic and copies ran while one was open for 0% -> 0% of each run, Pallas kernels for 31% -> 34%
where the time goes in v3:
time: 35.4 us
  Pallas kernels  31.4 us (89%)
  starting transfers between devices  2.47 us (7%)
  other arithmetic  0.74 us (2%)
  between operations  0.69 us (2%)
    pallas_call x1, Pallas kernels, local_step(): pl.pallas_call(weight_kernel, out_shape=(shape((n_loc, dim, ffn), F32), s...  12 us
    pallas_call x1, Pallas kernels, local_step(): pl.pallas_call(chain_kernel, out_shape=(shape((tok, dim), F32),) * 4 + (s...  9.97 us
    pallas_call x1, Pallas kernels, local_step(): pl.pallas_call(comm_kernel, out_shape=(shape((n_loc, 4, cap, dim), BF16),...  9.49 us
    ppermute x1, starting transfers between devices, local_step(): got_f = lax.ppermute(p_far, 'ep', pairs[1])  1.75 us
    convert_element_type x1, other arithmetic, local_step(): grad_x = (p_own + got_p + got_f + got_fp).astype(BF16)  0.74 us
  transfers between devices with their start and end apart: 3, of which 0 were waited for; matrix products, arithmetic and copies ran while one was open for 0% of the time, Pallas kernels for 34%

profile of v3, /device:TPU:0, one launch (start us, length us, event | category | flops | bytes accessed | tf_op | source)
XLA Modules:
  0.0 35.4 jit_solution(6896792605268744941)
XLA Ops:
  0.6 9.5 %comm_kernel.1 = (bf16[8,4,32,1024]{3,2,1,0:T(8,128)(2,1)S(1)}, bf16[8,128,512]{2,1,0:T(8,128)(2,1)S(1)}, f32[8,128,512]{2,1,0:T(8,128)S(1)}, f32[8,128,512]{2,1...) custom-call(bf16[64,1024]{1,0:T(8,128)(2,1)} %gy.1, ...), custom_call_target="tpu_custom_call" | custom-call | flops 1000000000 | bytes 30000000 | tf_op jit(solution)/shard_map/comm_kernel/pallas_call | solution.py:254
  10.1 0.0 copy-start
  10.1 10.0 %chain_kernel.1 = (f32[64,1024]{1,0:T(8,128)S(1)}, f32[64,1024]{1,0:T(8,128)S(1)}, f32[64,1024]{1,0:T(8,128)S(1)}, f32[64,1024]{1,0:T(8,128)S(1)}, bf16[8,128,10...) custom-call(bf16[8,4,32,1024]{3,2,1,0:T(8,128)(2,1)S(1)} %get-tuple-element.23.dd, ...), custom_call_target="tpu_custom_call" | custom-call | flops 4000000000 | bytes 20000000 | tf_op jit(solution)/shard_map/chain_kernel/pallas_call | solution.py:270
  20.1 0.6 %collective-permute-start = (f32[64,1024]{1,0:T(8,128)S(1)}, f32[64,1024]{1,0:T(8,128)S(1)}, u32[]{:S(2)}, u32[]{:S(2)}) collective-permute-start(f32[64,1024]{1,0:T(8,128)S(1)} %get-tuple-element.32), channel_id=1, source_target_pairs={{0,1},{1,0},{2,3},{3,2},{4,5},{5,4},{6,7},{7,6}} | collective-permute-start | bytes 786440 | tf_op jit(solution)/shard_map/ppermute | solution.py:284
  20.8 1.8 %collective-permute-start.1 = (f32[64,1024]{1,0:T(8,128)S(1)}, f32[64,1024]{1,0:T(8,128)S(1)}, u32[]{:S(2)}, u32[]{:S(2)}) collective-permute-start(f32[64,1024]{1,0:T(8,128)S(1)} %get-tuple-element.33), channel_id=1, source_target_pairs={{0,2},{1,3},{2,0},{3,1},{4,6},{5,7},{6,4},{7,5}} | collective-permute-start | bytes 786440 | tf_op jit(solution)/shard_map/ppermute | solution.py:283
  22.5 0.1 collective-permute-start.2
  22.6 0.0 copy-done
  22.6 12.0 %weight_kernel.1 = (f32[8,1024,512]{2,1,0:T(8,128)}, f32[8,1024,512]{2,1,0:T(8,128)}, f32[8,64]{1,0:T(8,128)}) custom-call(bf16[8,128,1024]{2,1,0:T(8,128)(2,1)S(1)} %copy-done, bf16[8,128,1024]{2,1,0:T(8,128)(2,1)S(1)} %get-tuple-element.35.dh, f32[8,64]{1,0:T(8,128)S(1)} %get-tuple-element.36.gg), custom_call_target="tpu_custom_call" | custom-call | flops 16000000000 | bytes 56000000 | tf_op jit(solution)/shard_map/weight_kernel/pallas_call | solution.py:286
  34.6 0.0 collective-permute-done
  34.6 0.0 collective-permute-done.1
  34.6 0.0 collective-permute-done.2
  34.6 0.7 %add_convert_fusion = bf16[64,1024]{1,0:T(8,128)(2,1)} fusion(f32[64,1024]{1,0:T(8,128)S(1)} %collective-permute-done.2, f32[64,1024]{1,0:T(8,128)S(1)} %collective-permute-done.1, f32[64,1024]{1,0:T(8,128)S(1)} %get-tuple-element.31, f32[64,1024]{1,0:T(8,128)S(1)} %collective-permute-done), kind=kLoop, calls=%fused_computation | loop fusion | flops 262144 | bytes 1179648 | tf_op jit(solution)/shard_map/convert_element_type | solution.py:296
Async XLA Ops:
  10.1 12.5 %copy-start = (bf16[8,128,1024]{2,1,0:T(8,128)(2,1)S(1)}, bf16[8,128,1024]{2,1,0:T(8,128)(2,1)}, u32[]{:S(2)}) copy-start(bf16[8,128,1024]{2,1,0:T(8,128)(2,1)} %x.1) | copy-start | bytes 6291460
  20.1 14.5 %collective-permute-start = (f32[64,1024]{1,0:T(8,128)S(1)}, f32[64,1024]{1,0:T(8,128)S(1)}, u32[]{:S(2)}, u32[]{:S(2)}) collective-permute-start(f32[64,1024]{1,0:T(8,128)S(1)} %get-tuple-element.32), channel_id=1, source_target_pairs={{0,1},{1,0},{2,3},{3,2},{4,5},{5,4},{6,7},{7,6}} | collective-permute-start | bytes 786440 | tf_op jit(solution)/shard_map/ppermute | solution.py:284
  20.8 13.8 %collective-permute-start.1 = (f32[64,1024]{1,0:T(8,128)S(1)}, f32[64,1024]{1,0:T(8,128)S(1)}, u32[]{:S(2)}, u32[]{:S(2)}) collective-permute-start(f32[64,1024]{1,0:T(8,128)S(1)} %get-tuple-element.33), channel_id=1, source_target_pairs={{0,2},{1,3},{2,0},{3,1},{4,6},{5,7},{6,4},{7,5}} | collective-permute-start | bytes 786440 | tf_op jit(solution)/shard_map/ppermute | solution.py:283
  22.5 12.1 %collective-permute-start.2 = (f32[64,1024]{1,0:T(8,128)S(1)}, f32[64,1024]{1,0:T(8,128)S(1)}, u32[]{:S(2)}, u32[]{:S(2)}) collective-permute-start(f32[64,1024]{1,0:T(8,128)S(1)} %get-tuple-element.34), channel_id=1, source_target_pairs={{0,3},{1,2},{2,1},{3,0},{4,7},{5,6},{6,5},{7,4}} | collective-permute-start | bytes 786440 | tf_op jit(solution)/shard_map/ppermute | solution.py:282

commit v4 on v3

--- a/solution.py
+++ b/solution.py
@@ -84,7 +84,7 @@
             cols.append(jnp.sum(jnp.where(hit, gate_row, 0.0), axis=1, keepdims=True))
             hots.append(jnp.where(hit, 1.0, 0.0).astype(BF16))
         hot = jnp.concatenate(hots, axis=0)
-        p_all[s] = hot
+        p_all[s] = hot.astype(F32).T.astype(BF16)
         for n in range(0, dim, COLS):
             picked = jnp.dot(hot, gy_all[s, :, n:n + COLS], preferred_element_type=F32)
             for e in range(n_loc):
@@ -100,7 +100,7 @@
         h3 = hu_v[e].astype(F32)
         sig = jax.nn.sigmoid(h1)
         act = h1 * sig
-        aa[e] = (act * h3).astype(BF16)
+        aa[e] = (act * h3).T.astype(BF16)
         c1[e] = h3 * sig * (1.0 + h1 * (1.0 - sig))
         act_o[e] = act
         return carry
@@ -140,67 +140,74 @@
         c.wait_send()
 
 
-def mix(main, side):
-    done = 0
-    for k, work in enumerate(main):
-        work()
-        upto = len(side) * (k + 1) // len(main)
-        for extra in side[done:upto]:
-            extra()
-        done = upto
-
-
-def chain_kernel(dd, aa, c1, act, p_all, wg, wu, wd, wg_hbm, wu_hbm, p_own, p_partner, p_far, p_far_partner, dh, owd, r_all, buf_d, wg_l, wu_l, out_sem, in_sem):
+def chain_kernel(dd, aa, c1, act, p_all, wg, wu, wd, wg_hbm, wu_hbm, p_own, p_partner, p_far, p_far_partner, dh, owd, r_all, buf_d, wg_l, wu_l, out_sem, in_sem, tail_sem):
     n_loc, _, cap, dim = dd.shape
-    ffn = aa.shape[2]
+    ffn = aa.shape[1]
     early = wg.shape[0]
     pairs = n_loc // 2
     ins = [pltpu.make_async_copy(wg_hbm.at[pl.ds(early, LATE)], wg_l, in_sem.at[0]), pltpu.make_async_copy(wu_hbm.at[pl.ds(early, LATE)], wu_l, in_sem.at[1])]
     for c in ins:
         c.start()
 
-    def first(e, n):
-        def work():
-            da = lax.dot_general(dd[e].reshape(4 * cap, dim), wd[e, n:n + COLS], NT, preferred_element_type=F32).astype(BF16).astype(F32)
+    def first(ea, eb, n, side):
+        acc = [None] * 2
+        for k in range(0, dim, COLS):
+            terms = [lax.dot_general(dd[e, :, :, k:k + COLS].reshape(4 * cap, COLS), wd[e, n:n + COLS, k:k + COLS], NT, preferred_element_type=F32) for e in (ea, eb)]
+            acc = [x if a is None else a + x for a, x in zip(acc, terms)]
+            for work in side[k // COLS]:
+                work()
+        for e, da in zip((ea, eb), acc):
+            da = da.astype(BF16).astype(F32)
             dh[e, :, n:n + COLS] = (da * c1[e, :, n:n + COLS]).astype(BF16)
             dh[e, :, ffn + n:ffn + n + COLS] = (da * act[e, :, n:n + COLS]).astype(BF16)
-        return work
-
-    def second(e, n):
-        def work():
-            g, u = (wg[e, n:n + COLS], wu[e, n:n + COLS]) if e < early else (wg_l[e - early, n:n + COLS], wu_l[e - early, n:n + COLS])
-            r = lax.dot_general(dh[e, :, :ffn], g, NT, preferred_element_type=F32) + lax.dot_general(dh[e, :, ffn:], u, NT, preferred_element_type=F32)
-            r = r.astype(BF16)
+
+    def gate_up_weight(e, n, k):
+        ref = (wg, wu) if e < early else (wg_l, wu_l)
+        return ref[k // ffn][e if e < early else e - early, n:n + COLS, k % ffn:k % ffn + COLS]
+
+    def second(ea, eb, na, nb):
+        acc = [None] * 4
+        for k in range(0, 2 * ffn, COLS):
+            terms = [lax.dot_general(dh[ea, :, k:k + COLS], gate_up_weight(ea, n, k), NT, preferred_element_type=F32) for n in (na, nb)]
+            terms += [lax.dot_general(gate_up_weight(eb, n, k), dh[eb, :, k:k + COLS], NT, preferred_element_type=F32) for n in (na, nb)]
+            acc = [x if a is None else a + x for a, x in zip(acc, terms)]
+        for i, n in enumerate((na, nb)):
+            ra = acc[i].astype(BF16)
+            rb = acc[2 + i].astype(BF16).T
             for s in range(4):
-                r_all[s, e, :, n:n + COLS] = r[s * cap:(s + 1) * cap]
-        return work
+                r_all[s, ea, :, n:n + COLS] = ra[s * cap:(s + 1) * cap]
+                r_all[s, eb, :, n:n + COLS] = rb[s * cap:(s + 1) * cap]
 
     def down(e, n, m):
         def work():
-            buf_d[(e // 2) % 2, e % 2, m:m + COLS, n:n + COLS] = lax.dot_general(aa[e, :, m:m + COLS], dd[e, :, :, n:n + COLS].reshape(4 * cap, COLS), TN, preferred_element_type=F32)
+            buf_d[(e // 2) % 2, e % 2, m:m + COLS, n:n + COLS] = jnp.dot(aa[e, m:m + COLS], dd[e, :, :, n:n + COLS].reshape(4 * cap, COLS), preferred_element_type=F32)
         return work
 
-    outs = [pltpu.make_async_copy(buf_d.at[p % 2], owd.at[pl.ds(2 * p, 2)], out_sem.at[p % 2]) for p in range(pairs)]
+    outs = [pltpu.make_async_copy(buf_d.at[p % 2], owd.at[pl.ds(2 * p, 2)], out_sem.at[p % 2]) for p in range(pairs - 1)]
+    tail = [pltpu.make_async_copy(buf_d.at[(pairs - 1) % 2, i], owd.at[n_loc - 2 + i], tail_sem.at[i]) for i in range(2)]
     for p in range(-1, pairs):
-        main, side = [], []
-        if p >= 0:
-            main += [second(2 * p + i, n) for n in range(0, dim, COLS) for i in range(2)]
-        if p + 1 < pairs:
-            main += [first(2 * p + 2 + i, n) for n in range(0, ffn, COLS) for i in range(2)]
-            side += [down(2 * p + 2 + i, n, m) for i in range(2) for n in range(0, dim, COLS) for m in range(0, ffn, COLS)]
-            if p >= 1:
-                outs[p - 1].wait()
-        else:
+        ea, eb = 2 * p, 2 * p + 1
+        if 1 <= p < pairs - 1:
+            outs[p - 1].wait()
+        if p == pairs - 1:
             for c in ins:
                 c.wait()
-        mix(main, side)
+        if p >= 0:
+            for n in range(0, dim, 2 * COLS):
+                second(ea, eb, n, n + COLS)
         if p + 1 < pairs:
-            outs[p + 1].start()
+            side = [down(ea + 2 + i, n, m) for i in range(2) for n in range(0, dim, COLS) for m in range(0, ffn, COLS)]
+            for h, n in enumerate(range(0, ffn, COLS)):
+                first(ea + 2, eb + 2, n, [side[8 * h + 2 * q:8 * h + 2 * q + 2] for q in range(4)])
+                if p + 2 == pairs:
+                    tail[h].start()
+            if p + 2 < pairs:
+                outs[p + 1].start()
 
     me, partner, far, far_partner = peer_ids()
     for s, ref in ((me, p_own), (partner, p_partner), (far, p_far), (far_partner, p_far_partner)):
-        ref[...] = lax.dot_general(p_all[s], r_all[s].reshape(n_loc * cap, dim), TN, preferred_element_type=F32)
-    for c in outs[-2:]:
+        ref[...] = jnp.dot(p_all[s], r_all[s].reshape(n_loc * cap, dim), preferred_element_type=F32)
+    for c in outs[-1:] + tail:
         c.wait()
 
 
@@ -253,8 +260,8 @@
         ins = [pltpu.with_memory_space_constraint(a, pltpu.HBM) for a in (grad_y, gate_vals.T, topk_idx.T, slot_ids.T, pair_counts, y_routed, h_gate, h_up, w_gate, w_up, w_down)]
         dd, aa, c1, act, p_all, wg_v, wu_v, wd_v, gg = pl.pallas_call(
             comm_kernel,
-            out_shape=(shape((n_loc, 4, cap, dim), BF16), shape((n_loc, rows, ffn), BF16), shape((n_loc, rows, ffn), F32), shape((n_loc, rows, ffn), F32),
-                       shape((4, n_loc * cap, tok), BF16), shape((n_loc - LATE, dim, ffn), BF16), shape((n_loc - LATE, dim, ffn), BF16), shape(w_down.shape, BF16), shape((top_k, tok), F32)),
+            out_shape=(shape((n_loc, 4, cap, dim), BF16), shape((n_loc, ffn, rows), BF16), shape((n_loc, rows, ffn), F32), shape((n_loc, rows, ffn), F32),
+                       shape((4, tok, n_loc * cap), BF16), shape((n_loc - LATE, dim, ffn), BF16), shape((n_loc - LATE, dim, ffn), BF16), shape(w_down.shape, BF16), shape((top_k, tok), F32)),
             in_specs=[hbm_spec] * 11,
             out_specs=(vmem_spec,) * 9,
             scratch_shapes=[
@@ -272,7 +279,7 @@
             out_shape=(shape((tok, dim), F32),) * 4 + (shape((n_loc, rows, 2 * ffn), BF16), shape((n_loc, ffn, dim), F32)),
             in_specs=[vmem_spec] * 8 + [hbm_spec] * 2,
             out_specs=(vmem_spec,) * 5 + (hbm_spec,),
-            scratch_shapes=[pltpu.VMEM((4, n_loc, cap, dim), BF16), pltpu.VMEM((2, 2, ffn, dim), F32), pltpu.VMEM((LATE, dim, ffn), BF16), pltpu.VMEM((LATE, dim, ffn), BF16), dma((2,)), dma((2,))],
+            scratch_shapes=[pltpu.VMEM((4, n_loc, cap, dim), BF16), pltpu.VMEM((2, 2, ffn, dim), F32), pltpu.VMEM((LATE, dim, ffn), BF16), pltpu.VMEM((LATE, dim, ffn), BF16), dma((2,)), dma((2,)), dma((2,))],
             compiler_params=pltpu.CompilerParams(vmem_limit_bytes=18 * MIB),
             cost_estimate=pl.CostEstimate(flops=4_000_000_000, bytes_accessed=20_000_000, transcendentals=0),
             name="chain_kernel",

time: 35.4 us -> 34.2 us (0.966)
  Pallas kernels: 31.4 us -> 30.2 us
    pallas_call x1, Pallas kernels: 9.97 us -> 8.72 us  [local_step(): pl.pallas_call(chain_kernel, out_shape=(shape((tok, dim), F32),) * 4 + (s...]
  transfers between devices with their start and end apart: 3 -> 3, of which waited for: 0 -> 0; matrix products, arithmetic and copies ran while one was open for 0% -> 0% of each run, Pallas kernels for 34% -> 35%
where the time goes in v4:
time: 34.2 us; the launch traced here: 34.1 us
  Pallas kernels  30.2 us (88%)
  starting transfers between devices  2.49 us (7%)
  other arithmetic  0.74 us (2%)
  between operations  0.69 us (2%)
    pallas_call x1, Pallas kernels, local_step(): pl.pallas_call(weight_kernel, out_shape=(shape((n_loc, dim, ffn), F32), s...  12 us
    pallas_call x1, Pallas kernels, local_step(): pl.pallas_call(comm_kernel, out_shape=(shape((n_loc, 4, cap, dim), BF16),...  9.49 us
    pallas_call x1, Pallas kernels, local_step(): pl.pallas_call(chain_kernel, out_shape=(shape((tok, dim), F32),) * 4 + (s...  8.72 us
    ppermute x1, starting transfers between devices, local_step(): got_f = lax.ppermute(p_far, 'ep', pairs[1])  1.77 us
    convert_element_type x1, other arithmetic, local_step(): grad_x = (p_own + got_p + got_f + got_fp).astype(BF16)  0.74 us
  transfers between devices with their start and end apart: 3, of which 0 were waited for; matrix products, arithmetic and copies ran while one was open for 0% of the time, Pallas kernels for 35%

profile of v4, /device:TPU:0, one launch (start us, length us, event | category | flops | bytes accessed | tf_op | source)
XLA Modules:
  0.0 34.1 jit_solution(2504245650904740201)
XLA Ops:
  0.6 9.5 %comm_kernel.1 = (bf16[8,4,32,1024]{3,2,1,0:T(8,128)(2,1)S(1)}, bf16[8,512,128]{2,1,0:T(8,128)(2,1)S(1)}, f32[8,128,512]{2,1,0:T(8,128)S(1)}, f32[8,128,512]{2,1...) custom-call(bf16[64,1024]{1,0:T(8,128)(2,1)} %gy.1, ...), custom_call_target="tpu_custom_call" | custom-call | flops 1000000000 | bytes 30000000 | tf_op jit(solution)/shard_map/comm_kernel/pallas_call | solution.py:261
  10.1 0.0 copy-start
  10.1 8.7 %chain_kernel.1 = (f32[64,1024]{1,0:T(8,128)S(1)}, f32[64,1024]{1,0:T(8,128)S(1)}, f32[64,1024]{1,0:T(8,128)S(1)}, f32[64,1024]{1,0:T(8,128)S(1)}, bf16[8,128,10...) custom-call(bf16[8,4,32,1024]{3,2,1,0:T(8,128)(2,1)S(1)} %get-tuple-element.23.dd, ...), custom_call_target="tpu_custom_call" | custom-call | flops 4000000000 | bytes 20000000 | tf_op jit(solution)/shard_map/chain_kernel/pallas_call | solution.py:277
  18.9 0.6 %collective-permute-start = (f32[64,1024]{1,0:T(8,128)S(1)}, f32[64,1024]{1,0:T(8,128)S(1)}, u32[]{:S(2)}, u32[]{:S(2)}) collective-permute-start(f32[64,1024]{1,0:T(8,128)S(1)} %get-tuple-element.32), channel_id=1, source_target_pairs={{0,1},{1,0},{2,3},{3,2},{4,5},{5,4},{6,7},{7,6}} | collective-permute-start | bytes 786440 | tf_op jit(solution)/shard_map/ppermute | solution.py:291
  19.5 1.8 %collective-permute-start.1 = (f32[64,1024]{1,0:T(8,128)S(1)}, f32[64,1024]{1,0:T(8,128)S(1)}, u32[]{:S(2)}, u32[]{:S(2)}) collective-permute-start(f32[64,1024]{1,0:T(8,128)S(1)} %get-tuple-element.33), channel_id=1, source_target_pairs={{0,2},{1,3},{2,0},{3,1},{4,6},{5,7},{6,4},{7,5}} | collective-permute-start | bytes 786440 | tf_op jit(solution)/shard_map/ppermute | solution.py:290
  21.3 0.1 collective-permute-start.2
  21.4 0.0 copy-done
  21.4 12.0 %weight_kernel.1 = (f32[8,1024,512]{2,1,0:T(8,128)}, f32[8,1024,512]{2,1,0:T(8,128)}, f32[8,64]{1,0:T(8,128)}) custom-call(bf16[8,128,1024]{2,1,0:T(8,128)(2,1)S(1)} %copy-done, bf16[8,128,1024]{2,1,0:T(8,128)(2,1)S(1)} %get-tuple-element.35.dh, f32[8,64]{1,0:T(8,128)S(1)} %get-tuple-element.36.gg), custom_call_target="tpu_custom_call" | custom-call | flops 16000000000 | bytes 56000000 | tf_op jit(solution)/shard_map/weight_kernel/pallas_call | solution.py:293
  33.4 0.0 collective-permute-done
  33.4 0.0 collective-permute-done.1
  33.4 0.0 collective-permute-done.2
  33.4 0.7 %add_convert_fusion = bf16[64,1024]{1,0:T(8,128)(2,1)} fusion(f32[64,1024]{1,0:T(8,128)S(1)} %collective-permute-done.2, f32[64,1024]{1,0:T(8,128)S(1)} %collective-permute-done.1, f32[64,1024]{1,0:T(8,128)S(1)} %get-tuple-element.31, f32[64,1024]{1,0:T(8,128)S(1)} %collective-permute-done), kind=kLoop, calls=%fused_computation | loop fusion | flops 262144 | bytes 1179648 | tf_op jit(solution)/shard_map/convert_element_type | solution.py:303
Async XLA Ops:
  10.1 11.2 %copy-start = (bf16[8,128,1024]{2,1,0:T(8,128)(2,1)S(1)}, bf16[8,128,1024]{2,1,0:T(8,128)(2,1)}, u32[]{:S(2)}) copy-start(bf16[8,128,1024]{2,1,0:T(8,128)(2,1)} %x.1) | copy-start | bytes 6291460
  18.9 14.5 %collective-permute-start = (f32[64,1024]{1,0:T(8,128)S(1)}, f32[64,1024]{1,0:T(8,128)S(1)}, u32[]{:S(2)}, u32[]{:S(2)}) collective-permute-start(f32[64,1024]{1,0:T(8,128)S(1)} %get-tuple-element.32), channel_id=1, source_target_pairs={{0,1},{1,0},{2,3},{3,2},{4,5},{5,4},{6,7},{7,6}} | collective-permute-start | bytes 786440 | tf_op jit(solution)/shard_map/ppermute | solution.py:291
  19.5 13.9 %collective-permute-start.1 = (f32[64,1024]{1,0:T(8,128)S(1)}, f32[64,1024]{1,0:T(8,128)S(1)}, u32[]{:S(2)}, u32[]{:S(2)}) collective-permute-start(f32[64,1024]{1,0:T(8,128)S(1)} %get-tuple-element.33), channel_id=1, source_target_pairs={{0,2},{1,3},{2,0},{3,1},{4,6},{5,7},{6,4},{7,5}} | collective-permute-start | bytes 786440 | tf_op jit(solution)/shard_map/ppermute | solution.py:290
  21.3 12.1 %collective-permute-start.2 = (f32[64,1024]{1,0:T(8,128)S(1)}, f32[64,1024]{1,0:T(8,128)S(1)}, u32[]{:S(2)}, u32[]{:S(2)}) collective-permute-start(f32[64,1024]{1,0:T(8,128)S(1)} %get-tuple-element.34), channel_id=1, source_target_pairs={{0,3},{1,2},{2,1},{3,0},{4,7},{5,6},{6,5},{7,4}} | collective-permute-start | bytes 786440 | tf_op jit(solution)/shard_map/ppermute | solution.py:289

commit v5 on v4

--- a/solution.py
+++ b/solution.py
@@ -43,7 +43,7 @@
     barrier = pltpu.get_barrier_semaphore()
     for d in peers:
         pl.semaphore_signal(barrier, inc=1, device_id={"ep": d}, device_id_type=MESH_ID)
-    bulk = [pltpu.make_async_copy(src, dst, bulk_sem.at[i]) for i, (src, dst) in enumerate(((hg, hg_v), (hu, hu_v), (yr, yr_v), (wd, wd_v), (wg.at[pl.ds(0, early)], wg_v), (wu.at[pl.ds(0, early)], wu_v)))]
+    bulk = [pltpu.make_async_copy(src, dst, bulk_sem.at[i]) for i, (src, dst) in enumerate(((hg, hg_v), (hu, hu_v), (yr, yr_v), (wd.at[pl.ds(0, early)], wd_v), (wg.at[pl.ds(0, early)], wg_v), (wu.at[pl.ds(0, early)], wu_v)))]
     for c in bulk:
         c.start(priority=1)
     for c in own:
@@ -58,7 +58,7 @@
     to_partner = remote(gy_all.at[me], gy_all.at[me], gs_sem.at[0], gr_sem.at[0], partner)
     for h in range(2):
         rows = pl.ds(h * half, half)
-        to_far.append(remote(gy_all.at[me, rows], gy_all.at[me, rows], gs_sem.at[1 + h], gr_sem.at[1 + h], far))
+        to_far.append(remote(gy_all.at[me, rows], gy_all.at[me, rows], gs_sem.at[1 + h], gr_sem.at[1 + h], far_partner))
     for i, d in enumerate(peers):
         for k, ref in enumerate((gv_all, tk_all, sl_all, pc_all)):
             small.append(remote(ref.at[me], ref.at[me], ss_sem.at[i, k], sr_sem.at[i, k], d))
@@ -122,17 +122,17 @@
     for h in range(2):
         rows = pl.ds(h * half, half)
         to_far[h].wait_recv()
-        c = remote(gy_all.at[far, rows], gy_all.at[far, rows], gs_sem.at[3 + h], gr_sem.at[3 + h], partner)
+        c = remote(gy_all.at[far_partner, rows], gy_all.at[far_partner, rows], gs_sem.at[3 + h], gr_sem.at[3 + h], partner)
         c.start()
         relay.append(c)
     for k in range(4):
+        small[8 + k].wait_recv()
+    build(far_partner)
+    for k in range(4):
         small[4 + k].wait_recv()
-    build(far)
-    for k in range(4):
-        small[8 + k].wait_recv()
     for h in range(2):
         relay[h].wait_recv()
-    build(far_partner)
+    build(far)
 
     for c in bulk[3:]:
         c.wait()
@@ -140,19 +140,22 @@
         c.wait_send()
 
 
-def chain_kernel(dd, aa, c1, act, p_all, wg, wu, wd, wg_hbm, wu_hbm, p_own, p_partner, p_far, p_far_partner, dh, owd, r_all, buf_d, wg_l, wu_l, out_sem, in_sem, tail_sem):
+def chain_kernel(dd, aa, c1, act, p_all, wg, wu, wd, wg_hbm, wu_hbm, wd_hbm, p_own, p_partner, p_far, p_far_partner, dh, owd, r_all, buf_d, wg_l, wu_l, wd_l, out_sem, in_sem, tail_sem):
     n_loc, _, cap, dim = dd.shape
     ffn = aa.shape[1]
     early = wg.shape[0]
     pairs = n_loc // 2
-    ins = [pltpu.make_async_copy(wg_hbm.at[pl.ds(early, LATE)], wg_l, in_sem.at[0]), pltpu.make_async_copy(wu_hbm.at[pl.ds(early, LATE)], wu_l, in_sem.at[1])]
+    ins = [pltpu.make_async_copy(wd_hbm.at[pl.ds(early, LATE)], wd_l, in_sem.at[2]), pltpu.make_async_copy(wg_hbm.at[pl.ds(early, LATE)], wg_l, in_sem.at[0]), pltpu.make_async_copy(wu_hbm.at[pl.ds(early, LATE)], wu_l, in_sem.at[1])]
     for c in ins:
         c.start()
+
+    def down_weight(e, n, k):
+        return wd[e, n:n + COLS, k:k + COLS] if e < early else wd_l[e - early, n:n + COLS, k:k + COLS]
 
     def first(ea, eb, n, side):
         acc = [None] * 2
         for k in range(0, dim, COLS):
-            terms = [lax.dot_general(dd[e, :, :, k:k + COLS].reshape(4 * cap, COLS), wd[e, n:n + COLS, k:k + COLS], NT, preferred_element_type=F32) for e in (ea, eb)]
+            terms = [lax.dot_general(dd[e, :, :, k:k + COLS].reshape(4 * cap, COLS), down_weight(e, n, k), NT, preferred_element_type=F32) for e in (ea, eb)]
             acc = [x if a is None else a + x for a, x in zip(acc, terms)]
             for work in side[k // COLS]:
                 work()
@@ -189,8 +192,10 @@
         ea, eb = 2 * p, 2 * p + 1
         if 1 <= p < pairs - 1:
             outs[p - 1].wait()
+        if p == pairs - 2:
+            ins[0].wait()
         if p == pairs - 1:
-            for c in ins:
+            for c in ins[1:]:
                 c.wait()
         if p >= 0:
             for n in range(0, dim, 2 * COLS):
@@ -211,33 +216,32 @@
         c.wait()
 
 
-def weight_kernel(x, dh, gg, owg, owu, ogg, buf_g, buf_u, out_sem):
-    n_loc = x.shape[0]
+def weight_kernel(x, dh, gg, owg, owu, ogg, buf, out_sem):
+    n_loc, _, dim = x.shape
     ffn = owg.shape[2]
+    half = dim // 2
     ogg[...] = gg[...]
 
-    def out_copies(e, slot):
-        return (pltpu.make_async_copy(buf_g.at[slot], owg.at[e], out_sem.at[slot, 0]),
-                pltpu.make_async_copy(buf_u.at[slot], owu.at[e], out_sem.at[slot, 1]))
+    def out_copy(e, slot, k):
+        out = (owg, owu)[k % 2]
+        rows = pl.ds(k // 2 * half, half)
+        return pltpu.make_async_copy(buf.at[slot, k], out.at[e, rows], out_sem.at[slot, k])
 
     def expert(e, carry):
         slot = lax.rem(e, 2)
-        c_g, c_u = out_copies(e, slot)
-
-        @pl.when(e >= 2)
-        def _():
-            for c in out_copies(e - 2, slot):
-                c.wait()
-        buf_g[slot] = lax.dot_general(x[e], dh[e, :, :ffn], TN, preferred_element_type=F32)
-        c_g.start()
-        buf_u[slot] = lax.dot_general(x[e], dh[e, :, ffn:], TN, preferred_element_type=F32)
-        c_u.start()
+        for k in range(4):
+            @pl.when(e >= 2)
+            def _():
+                out_copy(e - 2, slot, k).wait()
+            lhs = x[e, :, k // 2 * half:(k // 2 + 1) * half]
+            buf[slot, k] = lax.dot_general(lhs, dh[e, :, k % 2 * ffn:(k % 2 + 1) * ffn], TN, preferred_element_type=F32)
+            out_copy(e, slot, k).start()
         return carry
 
     lax.fori_loop(0, n_loc, expert, 0)
     for e in (n_loc - 2, n_loc - 1):
-        for c in out_copies(e, e % 2):
-            c.wait()
+        for k in range(4):
+            out_copy(e, e % 2, k).wait()
 
 
 def solution(mesh):
@@ -261,7 +265,7 @@
         dd, aa, c1, act, p_all, wg_v, wu_v, wd_v, gg = pl.pallas_call(
             comm_kernel,
             out_shape=(shape((n_loc, 4, cap, dim), BF16), shape((n_loc, ffn, rows), BF16), shape((n_loc, rows, ffn), F32), shape((n_loc, rows, ffn), F32),
-                       shape((4, tok, n_loc * cap), BF16), shape((n_loc - LATE, dim, ffn), BF16), shape((n_loc - LATE, dim, ffn), BF16), shape(w_down.shape, BF16), shape((top_k, tok), F32)),
+                       shape((4, tok, n_loc * cap), BF16), shape((n_loc - LATE, dim, ffn), BF16), shape((n_loc - LATE, dim, ffn), BF16), shape((n_loc - LATE, ffn, dim), BF16), shape((top_k, tok), F32)),
             in_specs=[hbm_spec] * 11,
             out_specs=(vmem_spec,) * 9,
             scratch_shapes=[
@@ -277,13 +281,13 @@
         p_own, p_partner, p_far, p_far_partner, dh, owd = pl.pallas_call(
             chain_kernel,
             out_shape=(shape((tok, dim), F32),) * 4 + (shape((n_loc, rows, 2 * ffn), BF16), shape((n_loc, ffn, dim), F32)),
-            in_specs=[vmem_spec] * 8 + [hbm_spec] * 2,
+            in_specs=[vmem_spec] * 8 + [hbm_spec] * 3,
             out_specs=(vmem_spec,) * 5 + (hbm_spec,),
-            scratch_shapes=[pltpu.VMEM((4, n_loc, cap, dim), BF16), pltpu.VMEM((2, 2, ffn, dim), F32), pltpu.VMEM((LATE, dim, ffn), BF16), pltpu.VMEM((LATE, dim, ffn), BF16), dma((2,)), dma((2,)), dma((2,))],
-            compiler_params=pltpu.CompilerParams(vmem_limit_bytes=18 * MIB),
+            scratch_shapes=[pltpu.VMEM((4, n_loc, cap, dim), BF16), pltpu.VMEM((2, 2, ffn, dim), F32), pltpu.VMEM((LATE, dim, ffn), BF16), pltpu.VMEM((LATE, dim, ffn), BF16), pltpu.VMEM((LATE, ffn, dim), BF16), dma((2,)), dma((3,)), dma((2,))],
+            compiler_params=pltpu.CompilerParams(vmem_limit_bytes=20 * MIB),
             cost_estimate=pl.CostEstimate(flops=4_000_000_000, bytes_accessed=20_000_000, transcendentals=0),
             name="chain_kernel",
-        )(dd, aa, c1, act, p_all, wg_v, wu_v, wd_v, ins[8], ins[9])
+        )(dd, aa, c1, act, p_all, wg_v, wu_v, wd_v, ins[8], ins[9], ins[10])
 
         pairs = [[(i, i ^ k) for i in range(4)] for k in (1, 2, 3)]
         got_fp = lax.ppermute(p_far_partner, "ep", pairs[2])
@@ -295,7 +299,7 @@
             out_shape=(shape((n_loc, dim, ffn), F32), shape((n_loc, dim, ffn), F32), shape((top_k, tok), F32)),
             in_specs=[vmem_spec] * 3,
             out_specs=(hbm_spec, hbm_spec, vmem_spec),
-            scratch_shapes=[pltpu.VMEM((2, dim, ffn), F32), pltpu.VMEM((2, dim, ffn), F32), dma((2, 2))],
+            scratch_shapes=[pltpu.VMEM((2, 4, dim // 2, ffn), F32), dma((2, 4))],
             compiler_params=pltpu.CompilerParams(vmem_limit_bytes=16 * MIB),
             cost_estimate=pl.CostEstimate(flops=16_000_000_000, bytes_accessed=56_000_000, transcendentals=0),
             name="weight_kernel",

time: 34.2 us -> 33.5 us (0.980)
  starting transfers between devices: 2.49 us -> 1.94 us
    ppermute x1, starting transfers between devices: 0.64 us -> 0.21 us  [local_step(): got_p = lax.ppermute(p_partner, 'ep', pairs[0])]
  transfers between devices with their start and end apart: 3 -> 3, of which waited for: 0 -> 0; matrix products, arithmetic and copies ran while one was open for 0% -> 0% of each run, Pallas kernels for 35% -> 36%
where the time goes in v5:
time: 33.5 us; the launch traced here: 33.4 us
  Pallas kernels  30.1 us (90%)
  starting transfers between devices  1.94 us (6%)
  other arithmetic  0.74 us (2%)
  between operations  0.69 us (2%)
    pallas_call x1, Pallas kernels, local_step(): pl.pallas_call(weight_kernel, out_shape=(shape((n_loc, dim, ffn), F32), s...  11.9 us
    pallas_call x1, Pallas kernels, local_step(): pl.pallas_call(comm_kernel, out_shape=(shape((n_loc, 4, cap, dim), BF16),...  9.42 us
    pallas_call x1, Pallas kernels, local_step(): pl.pallas_call(chain_kernel, out_shape=(shape((tok, dim), F32),) * 4 + (s...  8.77 us
    ppermute x1, starting transfers between devices, local_step(): got_f = lax.ppermute(p_far, 'ep', pairs[1])  1.65 us
    convert_element_type x1, other arithmetic, local_step(): grad_x = (p_own + got_p + got_f + got_fp).astype(BF16)  0.74 us
  transfers between devices with their start and end apart: 3, of which 0 were waited for; matrix products, arithmetic and copies ran while one was open for 0% of the time, Pallas kernels for 36%

profile of v5, /device:TPU:0, one launch (start us, length us, event | category | flops | bytes accessed | tf_op | source)
XLA Modules:
  0.0 33.4 jit_solution(17478871267443270357)
XLA Ops:
  0.6 9.4 %comm_kernel.1 = (bf16[8,4,32,1024]{3,2,1,0:T(8,128)(2,1)S(1)}, bf16[8,512,128]{2,1,0:T(8,128)(2,1)S(1)}, f32[8,128,512]{2,1,0:T(8,128)S(1)}, f32[8,128,512]{2,1...) custom-call(bf16[64,1024]{1,0:T(8,128)(2,1)} %gy.1, ...), custom_call_target="tpu_custom_call" | custom-call | flops 1000000000 | bytes 30000000 | tf_op jit(solution)/shard_map/comm_kernel/pallas_call | solution.py:265
  10.1 0.0 copy-start
  10.1 8.8 %chain_kernel.1 = (f32[64,1024]{1,0:T(8,128)S(1)}, f32[64,1024]{1,0:T(8,128)S(1)}, f32[64,1024]{1,0:T(8,128)S(1)}, f32[64,1024]{1,0:T(8,128)S(1)}, bf16[8,128,10...) custom-call(bf16[8,4,32,1024]{3,2,1,0:T(8,128)(2,1)S(1)} %get-tuple-element.23.dd, ...), custom_call_target="tpu_custom_call" | custom-call | flops 4000000000 | bytes 20000000 | tf_op jit(solution)/shard_map/chain_kernel/pallas_call | solution.py:281
  18.8 0.2 collective-permute-start
  19.1 1.7 %collective-permute-start.1 = (f32[64,1024]{1,0:T(8,128)S(1)}, f32[64,1024]{1,0:T(8,128)S(1)}, u32[]{:S(2)}, u32[]{:S(2)}) collective-permute-start(f32[64,1024]{1,0:T(8,128)S(1)} %get-tuple-element.33), channel_id=1, source_target_pairs={{0,2},{1,3},{2,0},{3,1},{4,6},{5,7},{6,4},{7,5}} | collective-permute-start | bytes 786440 | tf_op jit(solution)/shard_map/ppermute | solution.py:294
  20.7 0.1 collective-permute-start.2
  20.8 0.0 copy-done
  20.8 11.9 %weight_kernel.1 = (f32[8,1024,512]{2,1,0:T(8,128)}, f32[8,1024,512]{2,1,0:T(8,128)}, f32[8,64]{1,0:T(8,128)}) custom-call(bf16[8,128,1024]{2,1,0:T(8,128)(2,1)S(1)} %copy-done, bf16[8,128,1024]{2,1,0:T(8,128)(2,1)S(1)} %get-tuple-element.35.dh, f32[8,64]{1,0:T(8,128)S(1)} %get-tuple-element.36.gg), custom_call_target="tpu_custom_call" | custom-call | flops 16000000000 | bytes 56000000 | tf_op jit(solution)/shard_map/weight_kernel/pallas_call | solution.py:297
  32.7 0.0 collective-permute-done
  32.7 0.0 collective-permute-done.1
  32.7 0.0 collective-permute-done.2
  32.7 0.7 %add_convert_fusion = bf16[64,1024]{1,0:T(8,128)(2,1)} fusion(f32[64,1024]{1,0:T(8,128)S(1)} %collective-permute-done.2, f32[64,1024]{1,0:T(8,128)S(1)} %collective-permute-done.1, f32[64,1024]{1,0:T(8,128)S(1)} %get-tuple-element.31, f32[64,1024]{1,0:T(8,128)S(1)} %collective-permute-done), kind=kLoop, calls=%fused_computation | loop fusion | flops 262144 | bytes 1179648 | tf_op jit(solution)/shard_map/convert_element_type | solution.py:307
Async XLA Ops:
  10.1 10.7 %copy-start = (bf16[8,128,1024]{2,1,0:T(8,128)(2,1)S(1)}, bf16[8,128,1024]{2,1,0:T(8,128)(2,1)}, u32[]{:S(2)}) copy-start(bf16[8,128,1024]{2,1,0:T(8,128)(2,1)} %x.1) | copy-start | bytes 6291460
  18.8 13.8 %collective-permute-start = (f32[64,1024]{1,0:T(8,128)S(1)}, f32[64,1024]{1,0:T(8,128)S(1)}, u32[]{:S(2)}, u32[]{:S(2)}) collective-permute-start(f32[64,1024]{1,0:T(8,128)S(1)} %get-tuple-element.32), channel_id=1, source_target_pairs={{0,1},{1,0},{2,3},{3,2},{4,5},{5,4},{6,7},{7,6}} | collective-permute-start | bytes 786440 | tf_op jit(solution)/shard_map/ppermute | solution.py:295
  19.1 13.6 %collective-permute-start.1 = (f32[64,1024]{1,0:T(8,128)S(1)}, f32[64,1024]{1,0:T(8,128)S(1)}, u32[]{:S(2)}, u32[]{:S(2)}) collective-permute-start(f32[64,1024]{1,0:T(8,128)S(1)} %get-tuple-element.33), channel_id=1, source_target_pairs={{0,2},{1,3},{2,0},{3,1},{4,6},{5,7},{6,4},{7,5}} | collective-permute-start | bytes 786440 | tf_op jit(solution)/shard_map/ppermute | solution.py:294
  20.7 12.0 %collective-permute-start.2 = (f32[64,1024]{1,0:T(8,128)S(1)}, f32[64,1024]{1,0:T(8,128)S(1)}, u32[]{:S(2)}, u32[]{:S(2)}) collective-permute-start(f32[64,1024]{1,0:T(8,128)S(1)} %get-tuple-element.34), channel_id=1, source_target_pairs={{0,3},{1,2},{2,1},{3,0},{4,7},{5,6},{6,5},{7,4}} | collective-permute-start | bytes 786440 | tf_op jit(solution)/shard_map/ppermute | solution.py:293

commit v6 on v5

--- a/solution.py
+++ b/solution.py
@@ -140,7 +140,7 @@
         c.wait_send()
 
 
-def chain_kernel(dd, aa, c1, act, p_all, wg, wu, wd, wg_hbm, wu_hbm, wd_hbm, p_own, p_partner, p_far, p_far_partner, dh, owd, r_all, buf_d, wg_l, wu_l, wd_l, out_sem, in_sem, tail_sem):
+def chain_kernel(dd, aa, c1, act, p_all, wg, wu, wd, wg_hbm, wu_hbm, wd_hbm, p_own, p_partner, p_far, p_far_partner, dh, owd, r_lo, r_hi, buf_d, wg_l, wu_l, wd_l, out_sem, in_sem, tail_sem):
     n_loc, _, cap, dim = dd.shape
     ffn = aa.shape[1]
     early = wg.shape[0]
@@ -178,8 +178,10 @@
             ra = acc[i].astype(BF16)
             rb = acc[2 + i].astype(BF16).T
             for s in range(4):
-                r_all[s, ea, :, n:n + COLS] = ra[s * cap:(s + 1) * cap]
-                r_all[s, eb, :, n:n + COLS] = rb[s * cap:(s + 1) * cap]
+                r_half = r_lo if n < dim // 2 else r_hi
+                at = n % (dim // 2)
+                r_half[s, ea, :, at:at + COLS] = ra[s * cap:(s + 1) * cap]
+                r_half[s, eb, :, at:at + COLS] = rb[s * cap:(s + 1) * cap]
 
     def down(e, n, m):
         def work():
@@ -197,21 +199,21 @@
         if p == pairs - 1:
             for c in ins[1:]:
                 c.wait()
-        if p >= 0:
-            for n in range(0, dim, 2 * COLS):
-                second(ea, eb, n, n + COLS)
-        if p + 1 < pairs:
-            side = [down(ea + 2 + i, n, m) for i in range(2) for n in range(0, dim, COLS) for m in range(0, ffn, COLS)]
-            for h, n in enumerate(range(0, ffn, COLS)):
-                first(ea + 2, eb + 2, n, [side[8 * h + 2 * q:8 * h + 2 * q + 2] for q in range(4)])
+        side = [down(ea + 2 + i, n, m) for i in range(2) for n in range(0, dim, COLS) for m in range(0, ffn, COLS)] if p + 1 < pairs else []
+        for h in range(2):
+            if p >= 0:
+                second(ea, eb, 2 * h * COLS, (2 * h + 1) * COLS)
+            if p + 1 < pairs:
+                first(ea + 2, eb + 2, h * COLS, [side[8 * h + 2 * q:8 * h + 2 * q + 2] for q in range(4)])
                 if p + 2 == pairs:
                     tail[h].start()
-            if p + 2 < pairs:
-                outs[p + 1].start()
+        if p + 2 < pairs:
+            outs[p + 1].start()
 
     me, partner, far, far_partner = peer_ids()
-    for s, ref in ((me, p_own), (partner, p_partner), (far, p_far), (far_partner, p_far_partner)):
-        ref[...] = jnp.dot(p_all[s], r_all[s].reshape(n_loc * cap, dim), preferred_element_type=F32)
+    for k, r_half in enumerate((r_lo, r_hi)):
+        for s, ref in ((me, p_own), (partner, p_partner), (far, p_far), (far_partner, p_far_partner)):
+            ref[:, k * dim // 2:(k + 1) * dim // 2] = jnp.dot(p_all[s], r_half[s].reshape(n_loc * cap, dim // 2), preferred_element_type=F32)
     for c in outs[-1:] + tail:
         c.wait()
 
@@ -283,7 +285,7 @@
             out_shape=(shape((tok, dim), F32),) * 4 + (shape((n_loc, rows, 2 * ffn), BF16), shape((n_loc, ffn, dim), F32)),
             in_specs=[vmem_spec] * 8 + [hbm_spec] * 3,
             out_specs=(vmem_spec,) * 5 + (hbm_spec,),
-            scratch_shapes=[pltpu.VMEM((4, n_loc, cap, dim), BF16), pltpu.VMEM((2, 2, ffn, dim), F32), pltpu.VMEM((LATE, dim, ffn), BF16), pltpu.VMEM((LATE, dim, ffn), BF16), pltpu.VMEM((LATE, ffn, dim), BF16), dma((2,)), dma((3,)), dma((2,))],
+            scratch_shapes=[pltpu.VMEM((4, n_loc, cap, dim // 2), BF16), pltpu.VMEM((4, n_loc, cap, dim // 2), BF16), pltpu.VMEM((2, 2, ffn, dim), F32), pltpu.VMEM((LATE, dim, ffn), BF16), pltpu.VMEM((LATE, dim, ffn), BF16), pltpu.VMEM((LATE, ffn, dim), BF16), dma((2,)), dma((3,)), dma((2,))],
             compiler_params=pltpu.CompilerParams(vmem_limit_bytes=20 * MIB),
             cost_estimate=pl.CostEstimate(flops=4_000_000_000, bytes_accessed=20_000_000, transcendentals=0),
             name="chain_kernel",

time: 33.5 us -> 33.4 us (level)
  no operation moved by 1% of the time
where the time goes in v6:
time: 33.4 us; the launch traced here: 33.3 us
  Pallas kernels  30 us (90%)
  starting transfers between devices  1.94 us (6%)
  other arithmetic  0.74 us (2%)
  between operations  0.69 us (2%)
    pallas_call x1, Pallas kernels, local_step(): pl.pallas_call(weight_kernel, out_shape=(shape((n_loc, dim, ffn), F32), s...  11.9 us
    pallas_call x1, Pallas kernels, local_step(): pl.pallas_call(comm_kernel, out_shape=(shape((n_loc, 4, cap, dim), BF16),...  9.42 us
    pallas_call x1, Pallas kernels, local_step(): pl.pallas_call(chain_kernel, out_shape=(shape((tok, dim), F32),) * 4 + (s...  8.66 us
    ppermute x1, starting transfers between devices, local_step(): got_f = lax.ppermute(p_far, 'ep', pairs[1])  1.66 us
    convert_element_type x1, other arithmetic, local_step(): grad_x = (p_own + got_p + got_f + got_fp).astype(BF16)  0.74 us
  transfers between devices with their start and end apart: 3, of which 0 were waited for; matrix products, arithmetic and copies ran while one was open for 0% of the time, Pallas kernels for 36%

profile of v6, /device:TPU:0, one launch (start us, length us, event | category | flops | bytes accessed | tf_op | source)
XLA Modules:
  0.0 33.3 jit_solution(56007772824845570)
XLA Ops:
  0.6 9.4 %comm_kernel.1 = (bf16[8,4,32,1024]{3,2,1,0:T(8,128)(2,1)S(1)}, bf16[8,512,128]{2,1,0:T(8,128)(2,1)S(1)}, f32[8,128,512]{2,1,0:T(8,128)S(1)}, f32[8,128,512]{2,1...) custom-call(bf16[64,1024]{1,0:T(8,128)(2,1)} %gy.1, ...), custom_call_target="tpu_custom_call" | custom-call | flops 1000000000 | bytes 30000000 | tf_op jit(solution)/shard_map/comm_kernel/pallas_call | solution.py:267
  10.1 0.0 copy-start
  10.1 8.7 %chain_kernel.1 = (f32[64,1024]{1,0:T(8,128)S(1)}, f32[64,1024]{1,0:T(8,128)S(1)}, f32[64,1024]{1,0:T(8,128)S(1)}, f32[64,1024]{1,0:T(8,128)S(1)}, bf16[8,128,10...) custom-call(bf16[8,4,32,1024]{3,2,1,0:T(8,128)(2,1)S(1)} %get-tuple-element.23.dd, ...), custom_call_target="tpu_custom_call" | custom-call | flops 4000000000 | bytes 20000000 | tf_op jit(solution)/shard_map/chain_kernel/pallas_call | solution.py:283
  18.7 0.2 collective-permute-start
  18.9 1.7 %collective-permute-start.1 = (f32[64,1024]{1,0:T(8,128)S(1)}, f32[64,1024]{1,0:T(8,128)S(1)}, u32[]{:S(2)}, u32[]{:S(2)}) collective-permute-start(f32[64,1024]{1,0:T(8,128)S(1)} %get-tuple-element.33), channel_id=1, source_target_pairs={{0,2},{1,3},{2,0},{3,1},{4,6},{5,7},{6,4},{7,5}} | collective-permute-start | bytes 786440 | tf_op jit(solution)/shard_map/ppermute | solution.py:296
  20.6 0.1 collective-permute-start.2
  20.7 0.0 copy-done
  20.7 11.9 %weight_kernel.1 = (f32[8,1024,512]{2,1,0:T(8,128)}, f32[8,1024,512]{2,1,0:T(8,128)}, f32[8,64]{1,0:T(8,128)}) custom-call(bf16[8,128,1024]{2,1,0:T(8,128)(2,1)S(1)} %copy-done, bf16[8,128,1024]{2,1,0:T(8,128)(2,1)S(1)} %get-tuple-element.35.dh, f32[8,64]{1,0:T(8,128)S(1)} %get-tuple-element.36.gg), custom_call_target="tpu_custom_call" | custom-call | flops 16000000000 | bytes 56000000 | tf_op jit(solution)/shard_map/weight_kernel/pallas_call | solution.py:299
  32.6 0.0 collective-permute-done
  32.6 0.0 collective-permute-done.1
  32.6 0.0 collective-permute-done.2
  32.6 0.7 %add_convert_fusion = bf16[64,1024]{1,0:T(8,128)(2,1)} fusion(f32[64,1024]{1,0:T(8,128)S(1)} %collective-permute-done.2, f32[64,1024]{1,0:T(8,128)S(1)} %collective-permute-done.1, f32[64,1024]{1,0:T(8,128)S(1)} %get-tuple-element.31, f32[64,1024]{1,0:T(8,128)S(1)} %collective-permute-done), kind=kLoop, calls=%fused_computation | loop fusion | flops 262144 | bytes 1179648 | tf_op jit(solution)/shard_map/convert_element_type | solution.py:309
Async XLA Ops:
  10.1 10.6 %copy-start = (bf16[8,128,1024]{2,1,0:T(8,128)(2,1)S(1)}, bf16[8,128,1024]{2,1,0:T(8,128)(2,1)}, u32[]{:S(2)}) copy-start(bf16[8,128,1024]{2,1,0:T(8,128)(2,1)} %x.1) | copy-start | bytes 6291460
  18.7 13.8 %collective-permute-start = (f32[64,1024]{1,0:T(8,128)S(1)}, f32[64,1024]{1,0:T(8,128)S(1)}, u32[]{:S(2)}, u32[]{:S(2)}) collective-permute-start(f32[64,1024]{1,0:T(8,128)S(1)} %get-tuple-element.32), channel_id=1, source_target_pairs={{0,1},{1,0},{2,3},{3,2},{4,5},{5,4},{6,7},{7,6}} | collective-permute-start | bytes 786440 | tf_op jit(solution)/shard_map/ppermute | solution.py:297
  18.9 13.6 %collective-permute-start.1 = (f32[64,1024]{1,0:T(8,128)S(1)}, f32[64,1024]{1,0:T(8,128)S(1)}, u32[]{:S(2)}, u32[]{:S(2)}) collective-permute-start(f32[64,1024]{1,0:T(8,128)S(1)} %get-tuple-element.33), channel_id=1, source_target_pairs={{0,2},{1,3},{2,0},{3,1},{4,6},{5,7},{6,4},{7,5}} | collective-permute-start | bytes 786440 | tf_op jit(solution)/shard_map/ppermute | solution.py:296
  20.6 12.0 %collective-permute-start.2 = (f32[64,1024]{1,0:T(8,128)S(1)}, f32[64,1024]{1,0:T(8,128)S(1)}, u32[]{:S(2)}, u32[]{:S(2)}) collective-permute-start(f32[64,1024]{1,0:T(8,128)S(1)} %get-tuple-element.34), channel_id=1, source_target_pairs={{0,3},{1,2},{2,1},{3,0},{4,7},{5,6},{6,5},{7,4}} | collective-permute-start | bytes 786440 | tf_op jit(solution)/shard_map/ppermute | solution.py:295
